TPU v7x, 32 devices: a whole 2x2x4 slice. The times are simulated.
32 devices in a mesh: seq: 8 (over z, y), tp: 4 (over x, core).
Axes of the slice: x: 2, y: 2, z: 4, core: 2. Of those that a mesh axis runs over, the one named last changes fastest.
Arguments:
- encoded: bfloat16 [8192, 1280], P(('seq', 'tp')), may hold values from -6 to 6
- starts: int32 [32, 32], replicated, may hold values from 0 to 256, as said below
- w_up: bfloat16 [1280, 4096], P(None, 'tp'), may hold values from -0.15625 to 0.15625
- norm_gain: float32 [4096], replicated, may hold values from 0.25 to 1.75
- w_query: bfloat16 [4096, 4096], P(None, 'tp'), may hold values from -8 to 8
- w_key: bfloat16 [4096, 4096], P(None, 'tp'), may hold values from -8 to 8
- w_value: bfloat16 [4096, 4096], P(None, 'tp'), may hold values from -0.09375 to 0.09375
- w_out: bfloat16 [4096, 4096], P('tp'), may hold values from -0.09375 to 0.09375
- cotangent: bfloat16 [1024, 4096], P('seq', 'tp'), may hold values from -6 to 6
Outputs:
- latent_out: bfloat16 [1024, 4096], P('seq', 'tp')
- latent_grad: float32 [1024, 4096], P('seq', 'tp')
Inputs may be any that keep to these rules, and one draw needn't show every extreme that they name: `starts`: row i lists in increasing order the distinct offsets at which patches begin in byte shard i, followed by 256 in unused slots; every shard has at least one patch and at least 8, some shard exactly 32; shard 0 begins a patch at offset 0.
All inputs are finite; a program needn't handle non-finite values.
Results may differ from a plain program's by a relative error of at most 0.014.
Values may be sent and summed in bfloat16 or wider, within the bound.
A program may use at most 128 MiB of HBM per device.

v0:
```python
import functools

import jax
import jax.numpy as jnp
from jax import lax
from jax.experimental import pallas as pl
from jax.experimental.pallas import tpu as pltpu
from jax.sharding import PartitionSpec as P

HEAD_DIM = 128


EPS = 1e-05
NEG = -1e30
CONTRACT_LAST = (((1,), (1,)), ((), ()))


def shifted(block, axis, distance):
    devices = range(lax.axis_size(axis))
    route = [(i - distance, i) for i in devices if i - distance in devices]
    return lax.ppermute(block, axis, route)


def per_device(encoded, starts, w_up, norm_gain, w_query, w_key, w_value, w_out, cotangent):
    byte_rows = encoded.shape[0]
    patch_cap = starts.shape[1]
    model_width = norm_gain.shape[0]
    shard = lax.axis_index(("seq", "tp"))
    own_starts = lax.dynamic_slice_in_dim(starts, shard, 1, 0)[0]
    places = jnp.arange(byte_rows, dtype=jnp.int32)
    following = jnp.concatenate([own_starts[1:], jnp.full((1,), byte_rows, jnp.int32)])
    inside = (places[None, :] >= own_starts[:, None]) & (places[None, :] < following[:, None])
    sums = jnp.dot(inside.astype(jnp.bfloat16), encoded, preferred_element_type=jnp.float32)
    sizes = jnp.sum(inside.astype(jnp.float32), 1)
    leading = places[None, :] < own_starts[:1, None]
    lead_sum = jnp.dot(leading.astype(jnp.bfloat16), encoded, preferred_element_type=jnp.float32)
    lead_size = jnp.sum(leading.astype(jnp.float32), 1)
    next_sum, next_size = shifted((lead_sum, lead_size), ("seq", "tp"), -1)
    count = jnp.sum((own_starts < byte_rows).astype(jnp.int32))
    last_slot = (jnp.arange(patch_cap, dtype=jnp.int32) == count - 1).astype(jnp.float32)
    sums = sums + last_slot[:, None] * next_sum
    sizes = sizes + last_slot * next_size
    patches = (sums / jnp.maximum(sizes, 1.0)[:, None]).astype(jnp.bfloat16)
    group = lax.all_gather(patches, "tp", axis=0, tiled=True)
    latent_in = jnp.dot(group, w_up, preferred_element_type=jnp.float32).astype(jnp.bfloat16)
    group_rows, columns = latent_in.shape
    head_count = columns // HEAD_DIM
    wide_piece = lax.all_gather(latent_in, "tp", axis=1, tiled=True).astype(jnp.float32)
    scaled = (wide_piece * norm_gain[None, :]).astype(jnp.bfloat16)
    acc_query = jnp.dot(scaled, w_query, preferred_element_type=jnp.float32)
    acc_key = jnp.dot(scaled, w_key, preferred_element_type=jnp.float32)
    acc_value = jnp.dot(scaled, w_value, preferred_element_type=jnp.float32)
    acc_query, acc_key, acc_value, square = (
        acc_query,
        acc_key,
        acc_value,
        jnp.sum(wide_piece * wide_piece, 1),
    )
    rinv = lax.rsqrt(square / model_width + EPS)
    query = (rinv[:, None] * acc_query).astype(jnp.bfloat16)
    key_rows = (rinv[:, None] * acc_key).astype(jnp.bfloat16)
    value_rows = (rinv[:, None] * acc_value).astype(jnp.bfloat16)
    keys_all, values_all = (
        lax.all_gather(key_rows, "seq", axis=0, tiled=True),
        lax.all_gather(value_rows, "seq", axis=0, tiled=True),
    )
    patches_total = keys_all.shape[0]
    valid_all = (starts < byte_rows).reshape(patches_total)
    row_base = lax.axis_index("seq") * group_rows
    query_index = row_base + jnp.arange(group_rows, dtype=jnp.int32)
    key_index = jnp.arange(patches_total, dtype=jnp.int32)
    query_valid = lax.dynamic_slice_in_dim(valid_all, row_base, group_rows, 0)
    allowed = valid_all[None, :] & (key_index[None, :] <= query_index[:, None])
    scale = HEAD_DIM ** (-0.5)
    query_heads = query.reshape(group_rows, head_count, HEAD_DIM)
    key_heads = keys_all.reshape(patches_total, head_count, HEAD_DIM)
    value_heads = values_all.reshape(patches_total, head_count, HEAD_DIM)
    scores = (
        jnp.einsum("rhd,khd->hrk", query_heads, key_heads, preferred_element_type=jnp.float32)
        * scale
    )
    peak = jnp.max(jnp.where(allowed[None], scores, NEG), 2)
    expo = jnp.where(allowed[None], jnp.exp(scores - peak[:, :, None]), 0.0)
    total = jnp.sum(expo, 2)
    mixed = jnp.einsum(
        "hrk,khd->rhd", expo.astype(jnp.bfloat16), value_heads, preferred_element_type=jnp.float32
    )
    attn = (mixed / total.T[:, :, None]).astype(jnp.bfloat16)
    partial_value = jnp.dot(
        attn.reshape(group_rows, columns), w_out, preferred_element_type=jnp.float32
    )
    head_sum = lax.psum_scatter(
        partial_value.astype(jnp.bfloat16), "tp", scatter_dimension=1, tiled=True
    ).astype(jnp.float32)
    wide_in = latent_in.astype(jnp.float32)
    latent_out = jnp.where(query_valid[:, None], wide_in + head_sum, 0.0).astype(jnp.bfloat16)
    grad_out = jnp.where(query_valid[:, None], cotangent, jnp.zeros_like(cotangent))
    d_attn = lax.dot_general(
        lax.all_gather(grad_out, "tp", axis=1, tiled=True),
        w_out,
        CONTRACT_LAST,
        preferred_element_type=jnp.float32,
    ).astype(jnp.bfloat16)
    grad_heads = d_attn.reshape(group_rows, head_count, HEAD_DIM)
    delta = jnp.sum(grad_heads.astype(jnp.float32) * attn.astype(jnp.float32), 2).T
    probs = expo / total[:, :, None]
    d_probs = jnp.einsum(
        "rhd,khd->hrk", grad_heads, value_heads, preferred_element_type=jnp.float32
    )
    d_scores = (probs * (d_probs - delta[:, :, None])).astype(jnp.bfloat16)
    grad_query = (
        (
            jnp.einsum("hrk,khd->rhd", d_scores, key_heads, preferred_element_type=jnp.float32)
            * scale
        )
        .astype(jnp.bfloat16)
        .reshape(group_rows, columns)
    )
    weights_low = probs.astype(jnp.bfloat16)
    count_rows = group_rows * lax.axis_size("seq")
    key_part = jnp.einsum("hrk,rhd->khd", d_scores, query_heads, preferred_element_type=jnp.float32)
    value_part = jnp.einsum(
        "hrk,rhd->khd", weights_low, grad_heads, preferred_element_type=jnp.float32
    )
    both = lax.psum_scatter(
        jnp.concatenate(
            [key_part.reshape(count_rows, columns), value_part.reshape(count_rows, columns)], 1
        ).astype(jnp.bfloat16),
        "seq",
        scatter_dimension=0,
        tiled=True,
    ).astype(jnp.float32)
    grad_key = (both[:, :columns] * scale).astype(jnp.bfloat16)
    grad_value = both[:, columns:].astype(jnp.bfloat16)
    dnormed = (
        lax.dot_general(grad_query, w_query, CONTRACT_LAST, preferred_element_type=jnp.float32)
        + lax.dot_general(grad_key, w_key, CONTRACT_LAST, preferred_element_type=jnp.float32)
        + lax.dot_general(grad_value, w_value, CONTRACT_LAST, preferred_element_type=jnp.float32)
    )
    normed_grad = lax.psum_scatter(
        dnormed.astype(jnp.bfloat16), "tp", scatter_dimension=1, tiled=True
    ).astype(jnp.float32)
    gain_own = lax.dynamic_slice_in_dim(norm_gain, lax.axis_index("tp") * columns, columns, 0)
    dots = lax.psum(jnp.sum(gain_own[None, :] * normed_grad * wide_in, 1), "tp")
    latent_grad = (
        grad_out.astype(jnp.float32)
        + rinv[:, None] * gain_own[None, :] * normed_grad
        - wide_in * (rinv**3)[:, None] * dots[:, None] / model_width
    )
    return (latent_out, latent_grad)


MESH = pl.DeviceIdType.MESH


def block(ref, dim, index, size):
    at = pl.ds(pl.multiple_of(index * size, size), size)
    return ref.at[at, :] if dim == 0 else ref.at[:, at]


def greet(axis, me, n):
    barrier = pltpu.get_barrier_semaphore()
    for offset in range(1, n):
        pl.semaphore_signal(
            barrier, inc=1, device_id={axis: lax.rem(me + offset, n)}, device_id_type=MESH
        )
    pl.semaphore_wait(barrier, n - 1)


def swap_kernel(axis, n, count, src_dim, dst_dim, *refs):
    sources, targets = refs[:count], refs[count : 2 * count]
    send_sem, recv_sem, own_sem = refs[2 * count :]
    me = lax.axis_index(axis)
    greet(axis, me, n)
    copies = []
    for i in range(count):
        src_size = sources[i].shape[src_dim] // n
        dst_size = targets[i].shape[dst_dim] // n
        landing = block(targets[i], dst_dim, me, dst_size)
        for offset in range(1, n):
            peer = lax.rem(me + offset, n)
            copy = pltpu.make_async_remote_copy(
                src_ref=block(sources[i], src_dim, peer, src_size),
                dst_ref=landing,
                send_sem=send_sem.at[i, offset],
                recv_sem=recv_sem.at[i, offset],
                device_id={axis: peer},
                device_id_type=MESH,
            )
            copy.start()
            copies.append(copy)
        own = pltpu.make_async_copy(
            block(sources[i], src_dim, me, src_size), landing, own_sem.at[i]
        )
        own.start()
        copies.append(own)
    for copy in copies:
        copy.wait()


def swap(arrays, axis, src_dim, dst_dim, collective_id):
    n, count = lax.axis_size(axis), len(arrays)
    shapes = []
    for array in arrays:
        shape = list(array.shape)
        shape[src_dim] //= n
        shape[dst_dim] *= n
        shapes.append(jax.ShapeDtypeStruct(tuple(shape), array.dtype))
    return pl.pallas_call(
        functools.partial(swap_kernel, axis, n, count, src_dim, dst_dim),
        out_shape=shapes,
        in_specs=[pl.BlockSpec(memory_space=pltpu.VMEM)] * count,
        out_specs=[pl.BlockSpec(memory_space=pltpu.VMEM)] * count,
        scratch_shapes=[
            pltpu.SemaphoreType.DMA((count, n)),
            pltpu.SemaphoreType.DMA((count, n)),
            pltpu.SemaphoreType.DMA((count,)),
        ],
        compiler_params=pltpu.CompilerParams(
            collective_id=collective_id, has_side_effects=True
        ),
    )(*arrays)


def collect_kernel(axis, n, count, dim, *refs):
    sources, targets = refs[:count], refs[count : 2 * count]
    send_sem, recv_sem, own_sem = refs[2 * count :]
    me = lax.axis_index(axis)
    partner = me + 1 - 2 * lax.rem(me, 2)
    half = n // 2
    greet(axis, me, n)

    def send(i, src, dst, slot, peer):
        copy = pltpu.make_async_remote_copy(
            src_ref=src,
            dst_ref=dst,
            send_sem=send_sem.at[i, slot],
            recv_sem=recv_sem.at[i, slot],
            device_id={axis: peer},
            device_id_type=MESH,
        )
        copy.start()
        return copy

    far, near = [], []
    for i in range(count):
        size = sources[i].shape[dim]
        for step in range(1, half):
            peer = lax.rem(me + 2 * step, n)
            landing = block(targets[i], dim, me, size)
            far.append((i, step, send(i, sources[i], landing, step, peer)))
    for i in range(count):
        landing = block(targets[i], dim, me, sources[i].shape[dim])
        near.append(send(i, sources[i], landing, 0, partner))
        own = pltpu.make_async_copy(sources[i], landing, own_sem.at[i])
        own.start()
        near.append(own)
    for i, step, copy in far:
        copy.wait_recv()
        origin = lax.rem(me + n - 2 * step, n)
        arrived = block(targets[i], dim, origin, sources[i].shape[dim])
        near.append(send(i, arrived, arrived, half + step, partner))
    for _, _, copy in far:
        copy.wait_send()
    for copy in near:
        copy.wait()


def collect(arrays, axis, dim, collective_id):
    n, count = lax.axis_size(axis), len(arrays)
    shapes = []
    for array in arrays:
        shape = list(array.shape)
        shape[dim] *= n
        shapes.append(jax.ShapeDtypeStruct(tuple(shape), array.dtype))
    return pl.pallas_call(
        functools.partial(collect_kernel, axis, n, count, dim),
        out_shape=shapes,
        in_specs=[pl.BlockSpec(memory_space=pltpu.VMEM)] * count,
        out_specs=[pl.BlockSpec(memory_space=pltpu.VMEM)] * count,
        scratch_shapes=[
            pltpu.SemaphoreType.DMA((count, n)),
            pltpu.SemaphoreType.DMA((count, n)),
            pltpu.SemaphoreType.DMA((count,)),
        ],
        compiler_params=pltpu.CompilerParams(
            collective_id=collective_id, has_side_effects=True
        ),
    )(*arrays)


def one_head(query, keys, values, d_attn, allowed):
    scale = HEAD_DIM ** (-0.5)
    scores = lax.dot_general(query, keys, CONTRACT_LAST, preferred_element_type=jnp.float32)
    scores = scores * scale
    peak = jnp.max(jnp.where(allowed, scores, NEG), 1)
    expo = jnp.where(allowed, jnp.exp(scores - peak[:, None]), 0.0)
    total = jnp.sum(expo, 1)
    mixed = jnp.dot(expo.astype(jnp.bfloat16), values, preferred_element_type=jnp.float32)
    attn = (mixed / total[:, None]).astype(jnp.bfloat16)
    delta = jnp.sum(d_attn.astype(jnp.float32) * attn.astype(jnp.float32), 1)
    probs = expo / total[:, None]
    d_probs = lax.dot_general(d_attn, values, CONTRACT_LAST, preferred_element_type=jnp.float32)
    d_scores = (probs * (d_probs - delta[:, None])).astype(jnp.bfloat16)
    rows = (((0,), (0,)), ((), ()))
    grad_query = jnp.dot(d_scores, keys, preferred_element_type=jnp.float32) * scale
    grad_key = lax.dot_general(d_scores, query, rows, preferred_element_type=jnp.float32) * scale
    grad_value = lax.dot_general(
        probs.astype(jnp.bfloat16), d_attn, rows, preferred_element_type=jnp.float32
    )
    low = jnp.bfloat16
    return attn, grad_query.astype(low), grad_key.astype(low), grad_value.astype(low)


def per_device_heads(encoded, starts, w_up, norm_gain, w_query, w_key, w_value, w_out, cotangent):
    byte_rows = encoded.shape[0]
    patch_cap = starts.shape[1]
    model_width = norm_gain.shape[0]
    shard = lax.axis_index(("seq", "tp"))
    own_starts = lax.dynamic_slice_in_dim(starts, shard, 1, 0)[0]
    places = jnp.arange(byte_rows, dtype=jnp.int32)
    following = jnp.concatenate([own_starts[1:], jnp.full((1,), byte_rows, jnp.int32)])
    inside = (places[None, :] >= own_starts[:, None]) & (places[None, :] < following[:, None])
    sums = jnp.dot(inside.astype(jnp.bfloat16), encoded, preferred_element_type=jnp.float32)
    sizes = jnp.sum(inside.astype(jnp.float32), 1)
    leading = places[None, :] < own_starts[:1, None]
    lead_sum = jnp.dot(leading.astype(jnp.bfloat16), encoded, preferred_element_type=jnp.float32)
    lead_size = jnp.sum(leading.astype(jnp.float32), 1)
    next_sum, next_size = shifted((lead_sum, lead_size), ("seq", "tp"), -1)
    count = jnp.sum((own_starts < byte_rows).astype(jnp.int32))
    last_slot = (jnp.arange(patch_cap, dtype=jnp.int32) == count - 1).astype(jnp.float32)
    sums = sums + last_slot[:, None] * next_sum
    sizes = sizes + last_slot * next_size
    patches = (sums / jnp.maximum(sizes, 1.0)[:, None]).astype(jnp.bfloat16)
    (group,) = collect([patches], "tp", 0, 0)
    latent_in = jnp.dot(group, w_up, preferred_element_type=jnp.float32).astype(jnp.bfloat16)
    group_rows, columns = latent_in.shape
    valid_all = (starts < byte_rows).reshape(starts.size)
    row_base = lax.axis_index("seq") * group_rows
    query_valid = lax.dynamic_slice_in_dim(valid_all, row_base, group_rows, 0)
    grad_out = jnp.where(query_valid[:, None], cotangent, jnp.zeros_like(cotangent))
    wide_low, wide_grad = collect([latent_in, grad_out], "tp", 1, 1)
    wide_piece = wide_low.astype(jnp.float32)
    scaled = (wide_piece * norm_gain[None, :]).astype(jnp.bfloat16)
    rinv = lax.rsqrt(jnp.sum(wide_piece * wide_piece, 1) / model_width + EPS)

    def project(weight):
        acc = jnp.dot(scaled, weight, preferred_element_type=jnp.float32)
        return (rinv[:, None] * acc).astype(jnp.bfloat16)

    d_attn_rows = lax.dot_general(
        wide_grad, w_out, CONTRACT_LAST, preferred_element_type=jnp.float32
    ).astype(jnp.bfloat16)
    query, keys, values, d_attn = swap(
        [project(w_query), project(w_key), project(w_value), d_attn_rows], "seq", 1, 0, 2
    )
    index = jnp.arange(starts.size, dtype=jnp.int32)
    allowed = valid_all[None, :] & (index[None, :] <= index[:, None])
    pieces = []
    for start in range(0, query.shape[1], HEAD_DIM):
        cut = slice(start, start + HEAD_DIM)
        pieces.append(one_head(query[:, cut], keys[:, cut], values[:, cut], d_attn[:, cut], allowed))
    joined = [p[0] if len(p) == 1 else jnp.concatenate(p, 1) for p in zip(*pieces)]
    attn, grad_query, grad_key, grad_value = swap(joined, "seq", 0, 1, 3)
    partial_value = jnp.dot(attn, w_out, preferred_element_type=jnp.float32).astype(jnp.bfloat16)
    dnormed = (
        lax.dot_general(grad_query, w_query, CONTRACT_LAST, preferred_element_type=jnp.float32)
        + lax.dot_general(grad_key, w_key, CONTRACT_LAST, preferred_element_type=jnp.float32)
        + lax.dot_general(grad_value, w_value, CONTRACT_LAST, preferred_element_type=jnp.float32)
    ).astype(jnp.bfloat16)
    dot_parts = jnp.sum(norm_gain[None, :] * dnormed.astype(jnp.float32) * wide_piece, 1)
    tp_size = lax.axis_size("tp")
    dot_tile = jnp.broadcast_to(jnp.tile(dot_parts, tp_size)[None, :], (8, tp_size * group_rows))
    value_parts, grad_parts, dot_rows = swap([partial_value, dnormed, dot_tile], "tp", 1, 0, 4)
    dots = jnp.sum(dot_rows.reshape(tp_size, 8, group_rows)[:, 0], 0)

    def add_up(parts):
        return jnp.sum(parts.reshape(-1, group_rows, columns).astype(jnp.float32), 0)

    wide_in = latent_in.astype(jnp.float32)
    latent_out = jnp.where(query_valid[:, None], wide_in + add_up(value_parts), 0.0)
    normed_grad = add_up(grad_parts)
    gain_own = lax.dynamic_slice_in_dim(norm_gain, lax.axis_index("tp") * columns, columns, 0)
    latent_grad = (
        grad_out.astype(jnp.float32)
        + rinv[:, None] * gain_own[None, :] * normed_grad
        - wide_in * (rinv**3)[:, None] * dots[:, None] / model_width
    )
    return (latent_out.astype(jnp.bfloat16), latent_grad)


def solution(mesh):
    in_specs = (
        P(("seq", "tp"), None),
        P(),
        P(None, "tp"),
        P(),
        P(None, "tp"),
        P(None, "tp"),
        P(None, "tp"),
        P("tp", None),
        P("seq", "tp"),
    )
    out_specs = (P("seq", "tp"), P("seq", "tp"))

    def choose(*arrays):
        heads = arrays[4].shape[1] // HEAD_DIM
        whole_heads = heads % lax.axis_size("seq") == 0 and lax.axis_size("tp") % 2 == 0
        return (per_device_heads if whole_heads else per_device)(*arrays)

    return jax.shard_map(
        choose, mesh=mesh, in_specs=in_specs, out_specs=out_specs, check_vma=False
    )
```

profile of v0, /device:TPU:0, one launch (start us, length us, event | category | flops | bytes accessed | tf_op | source)
XLA Modules:
  0.0 190.4 jit_solution(18104906805008592816)
XLA Ops:
  0.7 1.5 fusion.41
  8.7 1.7 broadcast_select_fusion.refs_1_
  11.1 2.0 %divide_convert_fusion.refs_0_ = bf16[32,1280]{1,0:T(8,128)(2,1)} fusion(f32[32]{0:T(128)S(1)} %fusion.40, f32[1280]{0:T(1024)S(1)} %reduce.2, f32[32]{0:T(128)S(1)} %compare_convert_fusion.2, bf16[256,1280]{1,0:T(8,128)(2,1)} %param.9, s32[32]{0:T(128)S(1)} %pad_add_fusion, s32[32]{0:T(128)S(1)} %bitcast.56), kind=kOutput, calls=%fused_computation.46 | convolution fusion | flops 21159936 | bytes 742912 | tf_op jit(solution)/shard_map/dot_general | solution.py:324
  13.1 9.9 %shard_map.104 = bf16[128,1280]{1,0:T(8,128)(2,1)} custom-call(bf16[32,1280]{1,0:T(8,128)(2,1)} %divide_convert_fusion.refs_0_), custom_call_target="tpu_custom_call" | custom-call | tf_op jit(solution)/shard_map/pallas_call | solution.py:276
  23.1 2.2 %convolution_convert_fusion.2.refs_0_ = bf16[128,1024]{1,0:T(8,128)(2,1)} fusion(bf16[128,1280]{1,0:T(8,128)(2,1)} %shard_map.104, bf16[1280,1024]{1,0:T(8,128)(2,1)S(1)} %copy-done), kind=kOutput, calls=%fused_computation.36 | convolution fusion | flops 335675392 | bytes 3211264 | tf_op jit(solution)/shard_map/dot_general | solution.py:336
  25.2 18.0 %shard_map.105 = (bf16[128,4096]{1,0:T(8,128)(2,1)}, bf16[128,4096]{1,0:T(8,128)(2,1)}) custom-call(bf16[128,1024]{1,0:T(8,128)(2,1)} %convolution_convert_fusion.2.refs_0_, bf16[128,1024]{1,0:T(8,128)(2,1)} %broadcast_select_fusion.refs_1_), custom_call_target="tpu_custom_call" | custom-call | tf_op jit(solution)/shard_map/pallas_call | solution.py:276
  43.3 1.7 fusion.2
  45.0 5.8 %fusion.15.refs_0_ = bf16[128,1024]{1,0:T(8,128)(2,1)} fusion(bf16[4096,1024]{1,0:T(8,128)(2,1)} %param.13, bf16[128,4096]{1,0:T(8,128)(2,1)} %get-tuple-element.15, f32[4096]{0:T(1024)S(1)} %copy-done.4, f32[128]{0:T(128)S(1)} %get-tuple-element.33), kind=kOutput, calls=%fused_computation.29 | convolution fusion | flops 1075576832 | bytes 9716224 | tf_op jit(solution)/shard_map/dot_general | solution.py:348
  50.9 2.0 %fusion.16.refs_1_ = bf16[128,1024]{1,0:T(8,128)(2,1)} fusion(bf16[4096,1024]{1,0:T(8,128)(2,1)S(1)} %bitcast.44, bf16[128,4096]{1,0:T(8,128)(2,1)S(1)} %copy-done.1, f32[4096]{0:T(1024)S(1)} %copy-done.4, f32[128]{0:T(128)S(1)} %get-tuple-element.33), kind=kOutput, calls=%fused_computation.30 | convolution fusion | flops 1075576832 | bytes 9716224 | tf_op jit(solution)/shard_map/dot_general | solution.py:348
  53.2 2.0 %fusion.17.refs_2_ = bf16[128,1024]{1,0:T(8,128)(2,1)} fusion(bf16[4096,1024]{1,0:T(8,128)(2,1)S(1)} %bitcast.46, bf16[128,4096]{1,0:T(8,128)(2,1)S(1)} %copy-done.1, f32[4096]{0:T(1024)S(1)} %copy-done.4, f32[128]{0:T(128)S(1)} %get-tuple-element.33), kind=kOutput, calls=%fused_computation.31 | convolution fusion | flops 1075576832 | bytes 9716224 | tf_op jit(solution)/shard_map/dot_general | solution.py:348
  56.1 3.6 %convolution_convert_fusion.1.refs_3_ = bf16[128,1024]{1,0:T(8,128)(2,1)} fusion(bf16[128,4096]{1,0:T(8,128)(2,1)S(1)} %copy-done.5, bf16[1024,4096]{1,0:T(8,128)(2,1)S(1)} %bitcast.50), kind=kOutput, calls=%fused_computation.32 | convolution fusion | flops 1073872896 | bytes 9699328 | tf_op jit(solution)/shard_map/dot_general | solution.py:351
  59.6 31.7 %shard_map.106 = (bf16[1024,128]{1,0:T(8,128)(2,1)}, bf16[1024,128]{1,0:T(8,128)(2,1)}, bf16[1024,128]{1,0:T(8,128)(2,1)}, bf16[1024,128]{1,0:T(8,128)(2,1)}) custom-call(bf16[128,1024]{1,0:T(8,128)(2,1)} %fusion.15.refs_0_, bf16[128,1024]{1,0:T(8,128)(2,1)} %fusion.16.refs_1_, bf16[128,1024]{1,0:T(8,128)(2,1)} %fusion.17.refs_2_, ...), custom_call_target="tpu_custom_call" | custom-call | tf_op jit(solution)/shard_map/pallas_call | solution.py:209
  91.3 1.8 select_reduce_fusion
  93.2 2.0 %fusion.42 = f32[1024]{0:T(1024)S(1)} fusion(f32[1024]{0:T(1024)S(1)} %get-tuple-element.34, f32[1024,1024]{0,1:T(8,128)S(1)} %get-tuple-element.35, pred[1024]{0:T(1024)(128)(4,1)S(1)} %reshape.70), kind=kLoop, calls=%fused_computation.71 | loop fusion | flops 6290432 | bytes 4203520 | tf_op jit(solution)/shard_map/reduce_sum | solution.py:298
  95.2 1.7 multiply_reduce_fusion
  96.9 2.5 %multiply_convert_fusion = bf16[1024,1024]{0,1:T(8,128)(2,1)S(1)} fusion(bf16[1024,128]{1,0:T(8,128)(2,1)S(1)} %copy-done.10, bf16[1024,128]{1,0:T(8,128)(2,1)S(1)} %copy-done.13, f32[1024]{0:T(1024)S(1)} %get-tuple-element.36, f32[1024]{0:T(1024)S(1)} %fusion.42, f32[1024]{0:T(1024)S(1)} %get-tuple-element.34, f32[1024,1024]{0,1:T(8,128)S(1)} %get-tuple-element.35, ...), kind=kOutput, calls=%fused_computation.4 | convolution fusion | flops 277872640 | bytes 6829056 | tf_op jit(solution)/shard_map/dot_general | solution.py:303
  102.3 2.8 %fusion.12.refs_3_ = bf16[1024,128]{1,0:T(8,128)(2,1)} fusion(bf16[1024,128]{1,0:T(8,128)(2,1)S(1)} %copy-done.10, f32[1024]{0:T(1024)S(1)} %fusion.42, f32[1024,1024]{0,1:T(8,128)S(1)} %get-tuple-element.35, f32[1024]{0:T(1024)S(1)} %get-tuple-element.34, pred[1024]{0:T(1024)(128)(4,1)S(1)} %reshape.70), kind=kOutput, calls=%fused_computation.28 | convolution fusion | flops 275906560 | bytes 4727808 | tf_op jit(solution)/shard_map/dot_general | solution.py:308
  105.1 29.1 %shard_map.107 = (bf16[128,1024]{1,0:T(8,128)(2,1)}, bf16[128,1024]{1,0:T(8,128)(2,1)}, bf16[128,1024]{1,0:T(8,128)(2,1)}, bf16[128,1024]{1,0:T(8,128)(2,1)}) custom-call(bf16[1024,128]{1,0:T(8,128)(2,1)} %get-tuple-element.37.refs_0_, bf16[1024,128]{1,0:T(8,128)(2,1)} %fusion.18.refs_1_, bf16[1024,128]{1,0:T(8,128)(2,1)} %fusion.19.refs_2_, ...), custom_call_target="tpu_custom_call" | custom-call | tf_op jit(solution)/shard_map/pallas_call | solution.py:209
  134.2 5.8 %convolution_convert_fusion.refs_0_ = bf16[128,4096]{1,0:T(8,128)(2,1)} fusion(bf16[128,1024]{1,0:T(8,128)(2,1)} %get-tuple-element.21, bf16[1024,4096]{1,0:T(8,128)(2,1)} %param.16), kind=kOutput, calls=%fused_computation.3 | convolution fusion | flops 1074266112 | bytes 9699328 | tf_op jit(solution)/shard_map/dot_general | solution.py:365
  140.1 6.4 %fusion.44 = f32[128,4096]{1,0:T(8,128)S(1)} fusion(bf16[128,1024]{1,0:T(8,128)(2,1)S(1)} %copy-done.9, bf16[4096,1024]{1,0:T(8,128)(2,1)} %param.13), kind=kOutput, calls=%fused_computation.73 | convolution fusion | flops 1073741824 | bytes 10747904 | tf_op jit(solution)/shard_map/dot_general | solution.py:367
  146.5 6.4 %convolution_add_fusion.1 = f32[128,4096]{1,0:T(8,128)S(1)} fusion(f32[128,4096]{1,0:T(8,128)S(1)} %fusion.44, bf16[128,1024]{1,0:T(8,128)(2,1)S(1)} %copy-done.8, bf16[4096,1024]{1,0:T(8,128)(2,1)} %param.14), kind=kOutput, calls=%fused_computation.1 | convolution fusion | flops 1074266112 | bytes 12845056 | tf_op jit(solution)/shard_map/dot_general | solution.py:368
  153.0 4.0 %fusion.4 = (f32[128]{0:T(128)S(1)}, bf16[128,4096]{1,0:T(8,128)(2,1)}) fusion(bf16[128,4096]{1,0:T(8,128)(2,1)S(1)} %copy-done.2, f32[4096]{0:T(1024)S(1)} %copy-done.4, f32[128,4096]{1,0:T(8,128)S(1)} %convolution_add_fusion.1, bf16[128,1024]{1,0:T(8,128)(2,1)S(1)} %copy-done.7, bf16[4096,1024]{1,0:T(8,128)(2,1)S(1)} %bitcast.48), kind=kOutput, calls=%fused_computation.14 | convolution fusion | flops 1077411712 | bytes 12861952 | tf_op jit(solution)/shard_map/dot_general | solution.py:369
  157.6 28.7 %shard_map.108 = (bf16[512,1024]{1,0:T(8,128)(2,1)}, bf16[512,1024]{1,0:T(8,128)(2,1)}, f32[32,128]{1,0:T(8,128)}) custom-call(bf16[128,4096]{1,0:T(8,128)(2,1)} %convolution_convert_fusion.refs_0_, bf16[128,4096]{1,0:T(8,128)(2,1)} %get-tuple-element.39.refs_1_, f32[8,512]{1,0:T(8,128)} %broadcast_in_dim.32.refs_2_), custom_call_target="tpu_custom_call" | custom-call | tf_op jit(solution)/shard_map/pallas_call | solution.py:209
  187.1 2.1 %convert_reduce_fusion = (f32[128,1024]{1,0:T(8,128)S(1)}, f32[128,1024]{1,0:T(8,128)S(1)}) fusion(bf16[4,128,1024]{2,1,0:T(8,128)(2,1)} %bitcast.52, bf16[4,128,1024]{2,1,0:T(8,128)(2,1)} %bitcast.51), kind=kLoop, calls=%fused_computation.15 | loop fusion | flops 1835008 | bytes 3145728 | tf_op jit(solution)/shard_map/reduce_sum | solution.py:378
  (74 shorter events, 13.2 us)
Async XLA Ops:
  0.6 22.4 %copy-start = (bf16[1280,1024]{1,0:T(8,128)(2,1)S(1)}, bf16[1280,1024]{1,0:T(8,128)(2,1)}, u32[]{:S(2)}) copy-start(bf16[1280,1024]{1,0:T(8,128)(2,1)} %param.11) | copy-start | bytes 7864324
  0.6 44.3 %copy-start.4 = (f32[4096]{0:T(1024)S(1)}, f32[4096]{0:T(1024)}, u32[]{:S(2)}) copy-start(f32[4096]{0:T(1024)} %param.12) | copy-start | bytes 49156
  2.8 7.6 %collective-permute-start.1 = (f32[1]{0:T(128)}, f32[1]{0:T(128)}, u32[]{:S(2)}, u32[]{:S(2)}) collective-permute-start(f32[1]{0:T(128)} %bitcast.3), channel_id=1, source_target_pairs={{1,0},{2,1},{3,2},{4,3},{5,4},{6,5},{7,6},{8,7},{9,8},{10,9},{11,1... | collective-permute-start | bytes 20 | tf_op jit(solution)/shard_map/ppermute | solution.py:21
  5.5 5.6 %collective-permute-start = (f32[1,1280]{1,0:T(1,128)S(1)}, f32[1,1280]{1,0:T(1,128)S(1)}, u32[]{:S(2)}, u32[]{:S(2)}) collective-permute-start(f32[1,1280]{1,0:T(1,128)S(1)} %fusion.43), channel_id=1, source_target_pairs={{1,0},{2,1},{3,2},{4,3},{5,4},{6,5},{7,6},{8,7},{9,8},{10,9},{11,1... | collective-permute-start | bytes 15368 | tf_op jit(solution)/shard_map/ppermute | solution.py:21
  43.3 7.5 %slice-start = ((s8[8388608]{0:T(1024)(128)(4,1)}), s8[4194304]{0:T(1024)(128)(4,1)S(1)}, s32[]{:S(2)}) async-start(s8[8388608]{0:T(1024)(128)(4,1)} %bitcast.43), calls=%async_computation | async-start | bytes 8388608
  45.0 5.9 %slice-start.1 = ((s8[8388608]{0:T(1024)(128)(4,1)}), s8[4194304]{0:T(1024)(128)(4,1)S(1)}, s32[]{:S(2)}) async-start(s8[8388608]{0:T(1024)(128)(4,1)} %bitcast.43), calls=%async_computation.1 | async-start | bytes 8388608
  45.0 5.8 %copy-start.1 = (bf16[128,4096]{1,0:T(8,128)(2,1)S(1)}, bf16[128,4096]{1,0:T(8,128)(2,1)}, u32[]{:S(2)}) copy-start(bf16[128,4096]{1,0:T(8,128)(2,1)} %get-tuple-element.15) | copy-start | bytes 3145732
  45.0 7.9 %slice-start.2 = ((s8[8388608]{0:T(1024)(128)(4,1)}), s8[4194304]{0:T(1024)(128)(4,1)S(1)}, s32[]{:S(2)}) async-start(s8[8388608]{0:T(1024)(128)(4,1)} %bitcast.45), calls=%async_computation.2 | async-start | bytes 8388608
  50.8 2.4 %slice-start.3 = ((s8[8388608]{0:T(1024)(128)(4,1)}), s8[4194304]{0:T(1024)(128)(4,1)S(1)}, s32[]{:S(2)}) async-start(s8[8388608]{0:T(1024)(128)(4,1)} %bitcast.45), calls=%async_computation.3 | async-start | bytes 8388608
  50.9 4.4 %slice-start.6 = ((s8[8388608]{0:T(1024)(128)(4,1)}), s8[4194304]{0:T(1024)(128)(4,1)S(1)}, s32[]{:S(2)}) async-start(s8[8388608]{0:T(1024)(128)(4,1)} %bitcast.49), calls=%async_computation.6 | async-start | bytes 8388608
  53.2 2.5 %slice-start.7 = ((s8[8388608]{0:T(1024)(128)(4,1)}), s8[4194304]{0:T(1024)(128)(4,1)S(1)}, s32[]{:S(2)}) async-start(s8[8388608]{0:T(1024)(128)(4,1)} %bitcast.49), calls=%async_computation.7 | async-start | bytes 8388608
  53.2 2.8 %copy-start.5 = (bf16[128,4096]{1,0:T(8,128)(2,1)S(1)}, bf16[128,4096]{1,0:T(8,128)(2,1)}, u32[]{:S(2)}) copy-start(bf16[128,4096]{1,0:T(8,128)(2,1)} %get-tuple-element.16) | copy-start | bytes 3145732
  91.3 3.8 %copy-start.10 = (bf16[1024,128]{1,0:T(8,128)(2,1)S(1)}, bf16[1024,128]{1,0:T(8,128)(2,1)}, u32[]{:S(2)}) copy-start(bf16[1024,128]{1,0:T(8,128)(2,1)} %get-tuple-element.20) | copy-start | bytes 786436
  91.3 3.8 %copy-start.13 = (bf16[1024,128]{1,0:T(8,128)(2,1)S(1)}, bf16[1024,128]{1,0:T(8,128)(2,1)}, u32[]{:S(2)}) copy-start(bf16[1024,128]{1,0:T(8,128)(2,1)} %get-tuple-element.19) | copy-start | bytes 786436
  96.9 2.5 %copy-start.12 = (bf16[1024,128]{1,0:T(8,128)(2,1)S(1)}, bf16[1024,128]{1,0:T(8,128)(2,1)}, u32[]{:S(2)}) copy-start(bf16[1024,128]{1,0:T(8,128)(2,1)} %get-tuple-element.18) | copy-start | bytes 786436
  134.2 5.8 %copy-start.9 = (bf16[128,1024]{1,0:T(8,128)(2,1)S(1)}, bf16[128,1024]{1,0:T(8,128)(2,1)}, u32[]{:S(2)}) copy-start(bf16[128,1024]{1,0:T(8,128)(2,1)} %get-tuple-element.22) | copy-start | bytes 786436
  140.1 6.4 %copy-start.8 = (bf16[128,1024]{1,0:T(8,128)(2,1)S(1)}, bf16[128,1024]{1,0:T(8,128)(2,1)}, u32[]{:S(2)}) copy-start(bf16[128,1024]{1,0:T(8,128)(2,1)} %get-tuple-element.23) | copy-start | bytes 786436
  140.1 12.9 %slice-start.4 = ((s8[8388608]{0:T(1024)(128)(4,1)}), s8[4194304]{0:T(1024)(128)(4,1)S(1)}, s32[]{:S(2)}) async-start(s8[8388608]{0:T(1024)(128)(4,1)} %bitcast.47), calls=%async_computation.4 | async-start | bytes 8388608
  146.5 6.5 %slice-start.5 = ((s8[8388608]{0:T(1024)(128)(4,1)}), s8[4194304]{0:T(1024)(128)(4,1)S(1)}, s32[]{:S(2)}) async-start(s8[8388608]{0:T(1024)(128)(4,1)} %bitcast.47), calls=%async_computation.5 | async-start | bytes 8388608
  146.5 6.5 %copy-start.2 = (bf16[128,4096]{1,0:T(8,128)(2,1)S(1)}, bf16[128,4096]{1,0:T(8,128)(2,1)}, u32[]{:S(2)}) copy-start(bf16[128,4096]{1,0:T(8,128)(2,1)} %get-tuple-element.15) | copy-start | bytes 3145732
  146.5 6.5 %copy-start.7 = (bf16[128,1024]{1,0:T(8,128)(2,1)S(1)}, bf16[128,1024]{1,0:T(8,128)(2,1)}, u32[]{:S(2)}) copy-start(bf16[128,1024]{1,0:T(8,128)(2,1)} %get-tuple-element.24) | copy-start | bytes 786436
  157.0 32.1 %copy-start.3 = (bf16[128,1024]{1,0:T(8,128)(2,1)S(1)}, bf16[128,1024]{1,0:T(8,128)(2,1)}, u32[]{:S(2)}) copy-start(bf16[128,1024]{1,0:T(8,128)(2,1)} %convolution_convert_fusion.2.refs_0_) | copy-start | bytes 786436
  157.0 32.1 %dynamic-slice-start = ((f32[4096]{0:T(1024)}, s32[]{:T(128)}), f32[1024]{0:T(1024)S(1)}, s32[]{:S(2)}) async-start(f32[4096]{0:T(1024)} %param.12, s32[]{:T(128)} %select_n.30), calls=%async_computation.8 | async-start | bytes 8704 | tf_op jit(solution)/shard_map/dynamic_slice | solution.py:383
  157.0 32.2 %copy-start.6 = (bf16[128,1024]{1,0:T(8,128)(2,1)S(1)}, bf16[128,1024]{1,0:T(8,128)(2,1)}, u32[]{:S(2)}) copy-start(bf16[128,1024]{1,0:T(8,128)(2,1)} %param.17) | copy-start | bytes 786436
  (1 other events, 1.5 us)
where the time goes:
time: 191 us; the launch traced here: 190 us
  Pallas kernels  117 us (61%)
  matrix products  53.3 us (28%)
  other arithmetic  13.2 us (7%)
  starting transfers between devices  2.58 us (1%)
  local copies, waits for them, and re-layouts  2.16 us (1%)
    pallas_call x3, Pallas kernels, swap(): pl.pallas_call(functools.partial(swap_kernel, axis, n, count, src_dim, ds...  89.5 us
    pallas_call x2, Pallas kernels, collect(): pl.pallas_call(functools.partial(collect_kernel, axis, n, count, dim), ou...  28 us
    dot_general x3, matrix products, project(): acc = jnp.dot(scaled, weight, preferred_element_type=jnp.float32)  9.79 us
    dot_general x1, matrix products, per_device_heads(): lax.dot_general(grad_key, w_key, CONTRACT_LAST, preferred_element_type=jn...  6.42 us
    dot_general x1, matrix products, per_device_heads(): lax.dot_general(grad_query, w_query, CONTRACT_LAST, preferred_element_typ...  6.38 us
    dot_general x1, matrix products, per_device_heads(): jnp.dot(attn, w_out, preferred_element_type=jnp.float32)  5.81 us
    dot_general x1, matrix products, per_device_heads(): lax.dot_general(grad_value, w_value, CONTRACT_LAST, preferred_element_typ...  4.03 us
  transfers between devices with their start and end apart: 2, of which 0 were waited for; matrix products, arithmetic and copies ran while one was open for 3% of the time, Pallas kernels for 0%

commit v1 on v0

v1 whole, which is shorter than its diff:
```python
import functools

import jax
import jax.numpy as jnp
from jax import lax
from jax.experimental import pallas as pl
from jax.experimental.pallas import tpu as pltpu
from jax.sharding import PartitionSpec as P

HEAD_DIM = 128


EPS = 1e-05
NEG = -1e30
CONTRACT_LAST = (((1,), (1,)), ((), ()))


def shifted(block, axis, distance):
    devices = range(lax.axis_size(axis))
    route = [(i - distance, i) for i in devices if i - distance in devices]
    return lax.ppermute(block, axis, route)


def per_device(encoded, starts, w_up, norm_gain, w_query, w_key, w_value, w_out, cotangent):
    byte_rows = encoded.shape[0]
    patch_cap = starts.shape[1]
    model_width = norm_gain.shape[0]
    shard = lax.axis_index(("seq", "tp"))
    own_starts = lax.dynamic_slice_in_dim(starts, shard, 1, 0)[0]
    places = jnp.arange(byte_rows, dtype=jnp.int32)
    following = jnp.concatenate([own_starts[1:], jnp.full((1,), byte_rows, jnp.int32)])
    inside = (places[None, :] >= own_starts[:, None]) & (places[None, :] < following[:, None])
    sums = jnp.dot(inside.astype(jnp.bfloat16), encoded, preferred_element_type=jnp.float32)
    sizes = jnp.sum(inside.astype(jnp.float32), 1)
    leading = places[None, :] < own_starts[:1, None]
    lead_sum = jnp.dot(leading.astype(jnp.bfloat16), encoded, preferred_element_type=jnp.float32)
    lead_size = jnp.sum(leading.astype(jnp.float32), 1)
    next_sum, next_size = shifted((lead_sum, lead_size), ("seq", "tp"), -1)
    count = jnp.sum((own_starts < byte_rows).astype(jnp.int32))
    last_slot = (jnp.arange(patch_cap, dtype=jnp.int32) == count - 1).astype(jnp.float32)
    sums = sums + last_slot[:, None] * next_sum
    sizes = sizes + last_slot * next_size
    patches = (sums / jnp.maximum(sizes, 1.0)[:, None]).astype(jnp.bfloat16)
    group = lax.all_gather(patches, "tp", axis=0, tiled=True)
    latent_in = jnp.dot(group, w_up, preferred_element_type=jnp.float32).astype(jnp.bfloat16)
    group_rows, columns = latent_in.shape
    head_count = columns // HEAD_DIM
    wide_piece = lax.all_gather(latent_in, "tp", axis=1, tiled=True).astype(jnp.float32)
    scaled = (wide_piece * norm_gain[None, :]).astype(jnp.bfloat16)
    acc_query = jnp.dot(scaled, w_query, preferred_element_type=jnp.float32)
    acc_key = jnp.dot(scaled, w_key, preferred_element_type=jnp.float32)
    acc_value = jnp.dot(scaled, w_value, preferred_element_type=jnp.float32)
    acc_query, acc_key, acc_value, square = (
        acc_query,
        acc_key,
        acc_value,
        jnp.sum(wide_piece * wide_piece, 1),
    )
    rinv = lax.rsqrt(square / model_width + EPS)
    query = (rinv[:, None] * acc_query).astype(jnp.bfloat16)
    key_rows = (rinv[:, None] * acc_key).astype(jnp.bfloat16)
    value_rows = (rinv[:, None] * acc_value).astype(jnp.bfloat16)
    keys_all, values_all = (
        lax.all_gather(key_rows, "seq", axis=0, tiled=True),
        lax.all_gather(value_rows, "seq", axis=0, tiled=True),
    )
    patches_total = keys_all.shape[0]
    valid_all = (starts < byte_rows).reshape(patches_total)
    row_base = lax.axis_index("seq") * group_rows
    query_index = row_base + jnp.arange(group_rows, dtype=jnp.int32)
    key_index = jnp.arange(patches_total, dtype=jnp.int32)
    query_valid = lax.dynamic_slice_in_dim(valid_all, row_base, group_rows, 0)
    allowed = valid_all[None, :] & (key_index[None, :] <= query_index[:, None])
    scale = HEAD_DIM ** (-0.5)
    query_heads = query.reshape(group_rows, head_count, HEAD_DIM)
    key_heads = keys_all.reshape(patches_total, head_count, HEAD_DIM)
    value_heads = values_all.reshape(patches_total, head_count, HEAD_DIM)
    scores = (
        jnp.einsum("rhd,khd->hrk", query_heads, key_heads, preferred_element_type=jnp.float32)
        * scale
    )
    peak = jnp.max(jnp.where(allowed[None], scores, NEG), 2)
    expo = jnp.where(allowed[None], jnp.exp(scores - peak[:, :, None]), 0.0)
    total = jnp.sum(expo, 2)
    mixed = jnp.einsum(
        "hrk,khd->rhd", expo.astype(jnp.bfloat16), value_heads, preferred_element_type=jnp.float32
    )
    attn = (mixed / total.T[:, :, None]).astype(jnp.bfloat16)
    partial_value = jnp.dot(
        attn.reshape(group_rows, columns), w_out, preferred_element_type=jnp.float32
    )
    head_sum = lax.psum_scatter(
        partial_value.astype(jnp.bfloat16), "tp", scatter_dimension=1, tiled=True
    ).astype(jnp.float32)
    wide_in = latent_in.astype(jnp.float32)
    latent_out = jnp.where(query_valid[:, None], wide_in + head_sum, 0.0).astype(jnp.bfloat16)
    grad_out = jnp.where(query_valid[:, None], cotangent, jnp.zeros_like(cotangent))
    d_attn = lax.dot_general(
        lax.all_gather(grad_out, "tp", axis=1, tiled=True),
        w_out,
        CONTRACT_LAST,
        preferred_element_type=jnp.float32,
    ).astype(jnp.bfloat16)
    grad_heads = d_attn.reshape(group_rows, head_count, HEAD_DIM)
    delta = jnp.sum(grad_heads.astype(jnp.float32) * attn.astype(jnp.float32), 2).T
    probs = expo / total[:, :, None]
    d_probs = jnp.einsum(
        "rhd,khd->hrk", grad_heads, value_heads, preferred_element_type=jnp.float32
    )
    d_scores = (probs * (d_probs - delta[:, :, None])).astype(jnp.bfloat16)
    grad_query = (
        (
            jnp.einsum("hrk,khd->rhd", d_scores, key_heads, preferred_element_type=jnp.float32)
            * scale
        )
        .astype(jnp.bfloat16)
        .reshape(group_rows, columns)
    )
    weights_low = probs.astype(jnp.bfloat16)
    count_rows = group_rows * lax.axis_size("seq")
    key_part = jnp.einsum("hrk,rhd->khd", d_scores, query_heads, preferred_element_type=jnp.float32)
    value_part = jnp.einsum(
        "hrk,rhd->khd", weights_low, grad_heads, preferred_element_type=jnp.float32
    )
    both = lax.psum_scatter(
        jnp.concatenate(
            [key_part.reshape(count_rows, columns), value_part.reshape(count_rows, columns)], 1
        ).astype(jnp.bfloat16),
        "seq",
        scatter_dimension=0,
        tiled=True,
    ).astype(jnp.float32)
    grad_key = (both[:, :columns] * scale).astype(jnp.bfloat16)
    grad_value = both[:, columns:].astype(jnp.bfloat16)
    dnormed = (
        lax.dot_general(grad_query, w_query, CONTRACT_LAST, preferred_element_type=jnp.float32)
        + lax.dot_general(grad_key, w_key, CONTRACT_LAST, preferred_element_type=jnp.float32)
        + lax.dot_general(grad_value, w_value, CONTRACT_LAST, preferred_element_type=jnp.float32)
    )
    normed_grad = lax.psum_scatter(
        dnormed.astype(jnp.bfloat16), "tp", scatter_dimension=1, tiled=True
    ).astype(jnp.float32)
    gain_own = lax.dynamic_slice_in_dim(norm_gain, lax.axis_index("tp") * columns, columns, 0)
    dots = lax.psum(jnp.sum(gain_own[None, :] * normed_grad * wide_in, 1), "tp")
    latent_grad = (
        grad_out.astype(jnp.float32)
        + rinv[:, None] * gain_own[None, :] * normed_grad
        - wide_in * (rinv**3)[:, None] * dots[:, None] / model_width
    )
    return (latent_out, latent_grad)


MESH = pl.DeviceIdType.MESH
LOW = jnp.bfloat16
WIDE = jnp.float32
ROWS_FIRST = (((0,), (0,)), ((), ()))


def tile_of(index, size):
    return pl.ds(pl.multiple_of(index * size, size), size)


def dot(a, b):
    return jnp.dot(a, b, preferred_element_type=WIDE)


def dot_last(a, b):
    return lax.dot_general(a, b, CONTRACT_LAST, preferred_element_type=WIDE)


def to_row(column):
    n = column.shape[0]
    down = lax.broadcasted_iota(jnp.int32, (n, n), 0)
    across = lax.broadcasted_iota(jnp.int32, (n, n), 1)
    return jnp.sum(jnp.where(down == across, column, 0.0), 0, keepdims=True)


def to_column(row, shift=0):
    n = row.shape[1]
    down = lax.broadcasted_iota(jnp.int32, (n, n), 0)
    across = lax.broadcasted_iota(jnp.int32, (n, n), 1)
    return jnp.sum(jnp.where(down + shift == across, row, 0.0), 1, keepdims=True)


def layer_kernel(
    seq_size,
    tp_size,
    encoded,
    starts,
    gain,
    cotangent,
    w_up_far,
    w_query_far,
    w_key_far,
    w_value_far,
    w_out_far,
    out_value,
    out_grad,
    w_up,
    w_query,
    w_key,
    w_value,
    w_out,
    lead_out,
    lead_in,
    group,
    wide,
    wide_grad,
    scaled,
    valid_column,
    rinv_column,
    outbox,
    heads,
    value_turned,
    key_turned,
    scores,
    d_probs,
    key_sum,
    value_sum,
    returns,
    back,
    grad_sum,
    partial,
    pair_in,
    cross_out,
    cross_in,
    dots_out,
    dots_in,
    weight_sem,
    lead_sem,
    gather_send,
    gather_recv,
    out_send,
    out_recv,
    back_send,
    back_recv,
    pair_send,
    pair_recv,
    cross_send,
    cross_recv,
    dots_send,
    dots_recv,
):
    byte_rows, byte_width = encoded.shape
    shards, cap = starts.shape
    rows, columns = cotangent.shape
    model_width = gain.shape[1]
    patches_total = shards * cap
    mine = lax.axis_index("seq")
    t = lax.axis_index("tp")
    chip, core = t // 2, lax.rem(t, 2)
    shard = mine * tp_size + t
    partner = t + 1 - 2 * core
    across = lax.rem(t + 2, tp_size)
    diagonal = lax.rem(partner + 2, tp_size)
    tile = 2 * HEAD_DIM
    tiles = columns // tile
    scale = HEAD_DIM ** (-0.5)

    def remote(src, dst, send, recv, device):
        return pltpu.make_async_remote_copy(
            src_ref=src,
            dst_ref=dst,
            send_sem=send,
            recv_sem=recv,
            device_id=device,
            device_id_type=MESH,
        )

    pieces = weight_sem.shape[1]

    def weight_copies(i, far, near):
        depth = far.shape[0] // pieces
        return [
            pltpu.make_async_copy(
                far.at[pl.ds(p * depth, depth)], near.at[pl.ds(p * depth, depth)], weight_sem.at[i, p]
            )
            for p in range(pieces)
        ]

    up_copies = weight_copies(0, w_up_far, w_up)
    out_copies = weight_copies(1, w_out_far, w_out)
    key_copies = weight_copies(2, w_key_far, w_key)
    query_copies = weight_copies(3, w_query_far, w_query)
    value_copies = weight_copies(4, w_value_far, w_value)
    for copies in (up_copies, out_copies, key_copies, query_copies, value_copies):
        for copy in copies:
            copy.start()

    barrier = pltpu.get_barrier_semaphore()
    for offset in range(1, tp_size):
        pl.semaphore_signal(
            barrier, inc=1, device_id={"tp": lax.rem(t + offset, tp_size)}, device_id_type=MESH
        )
    for offset in range(1, seq_size):
        pl.semaphore_signal(
            barrier, inc=1, device_id={"seq": lax.rem(mine + offset, seq_size)}, device_id_type=MESH
        )
    has_before = shard > 0
    has_after = shard < shards - 1
    group_first = jnp.logical_and(t == 0, has_before)
    group_last = jnp.logical_and(t == tp_size - 1, has_after)
    shard_before = {
        "seq": jnp.where(t == 0, lax.rem(mine + seq_size - 1, seq_size), mine),
        "tp": lax.rem(t + tp_size - 1, tp_size),
    }
    shard_after = {
        "seq": jnp.where(t == tp_size - 1, lax.rem(mine + 1, seq_size), mine),
        "tp": lax.rem(t + 1, tp_size),
    }

    @pl.when(group_first)
    def _():
        pl.semaphore_signal(barrier, inc=1, device_id=shard_before, device_id_type=MESH)

    @pl.when(group_last)
    def _():
        pl.semaphore_signal(barrier, inc=1, device_id=shard_after, device_id_type=MESH)

    limit = float(byte_rows)
    own = starts[pl.ds(shard, 1), :].astype(WIDE)
    after = starts[pl.ds(jnp.minimum(shard + 1, shards - 1), 1), :].astype(WIDE)
    first = to_column(own)
    slot = lax.broadcasted_iota(jnp.int32, (cap, 1), 0)
    following = to_column(own, 1) + jnp.where(slot == cap - 1, limit, 0.0)
    places = lax.broadcasted_iota(jnp.int32, (cap, byte_rows), 1).astype(WIDE)
    inside = jnp.where((places >= first) & (places < following), 1.0, 0.0).astype(LOW)
    lead_places = lax.broadcasted_iota(jnp.int32, (16, byte_rows), 1).astype(WIDE)
    leading = jnp.where(lead_places < own[:, :1], 1.0, 0.0).astype(LOW)
    lead_out[...] = dot(leading, encoded[...])[:1]

    index = lax.broadcasted_iota(jnp.int32, (patches_total, shards), 0)
    lane = lax.broadcasted_iota(jnp.int32, (patches_total, shards), 1)
    owner = jnp.where((index >= lane * cap) & (index < lane * cap + cap), 1.0, 0.0).astype(LOW)
    valid = jnp.where(starts[...].astype(WIDE) < limit, 1.0, 0.0).astype(LOW)
    spread = dot(owner, valid)
    slots = lax.broadcasted_iota(jnp.int32, (patches_total, cap), 1)
    places_in = lax.broadcasted_iota(jnp.int32, (patches_total, cap), 0)
    valid_column[...] = jnp.sum(
        jnp.where(jnp.bitwise_and(places_in, cap - 1) == slots, spread, 0.0), 1, keepdims=True
    )
    own_rows = tile_of(mine, rows)
    row_valid = valid_column[own_rows, :]
    wide_grad[t] = jnp.where(row_valid > 0.5, cotangent[...].astype(WIDE), 0.0).astype(LOW)
    sums = dot(inside, encoded[...])

    neighbours = group_first.astype(jnp.int32) + group_last.astype(jnp.int32)
    pl.semaphore_wait(barrier, tp_size + seq_size - 2 + neighbours)

    lead_copy = remote(lead_out, lead_in, lead_sem.at[0], lead_sem.at[1], shard_before)

    @pl.when(has_before)
    def _():
        lead_copy.start()

    def gather_start(k, view):
        piece = view(t)
        remote(
            piece, piece, gather_send.at[0, k], gather_recv.at[0, k], {"tp": across}
        ).start()
        remote(
            piece, piece, gather_send.at[1, k], gather_recv.at[1, k], {"tp": partner}
        ).start()

    def gather_relay(k, view):
        piece = view(across)
        remote(
            piece, piece, gather_send.at[0, k], gather_recv.at[0, k], {"tp": across}
        ).wait_recv()
        remote(
            piece, piece, gather_send.at[2, k], gather_recv.at[2, k], {"tp": partner}
        ).start()

    def gather_finish(k, view):
        for way, origin in ((1, partner), (2, diagonal)):
            piece = view(origin)
            remote(
                piece, piece, gather_send.at[way, k], gather_recv.at[way, k], {"tp": partner}
            ).wait_recv()

    def gather_drain(k, view):
        for way, origin, target in ((0, t, across), (1, t, partner), (2, across, partner)):
            piece = view(origin)
            remote(
                piece, piece, gather_send.at[way, k], gather_recv.at[way, k], {"tp": target}
            ).wait_send()

    half_rows = rows // 2
    grad_views = [
        lambda q, p=p: wide_grad.at[q, pl.ds(p * half_rows, half_rows)] for p in range(2)
    ]
    group_view = lambda q: group.at[tile_of(q, cap)]

    def wide_view(j):
        return lambda q: wide.at[q, :, tile_of(j, tile)]

    gather_start(1, grad_views[0])

    @pl.when(has_after)
    def _():
        lead_copy.wait_recv()

    joined = jnp.where(
        jnp.logical_and(first < limit, following >= limit), jnp.where(has_after, 1.0, 0.0), 0.0
    )
    sums = sums + joined * jnp.where(has_after, lead_in[...], 0.0)
    sizes = (following - first) * jnp.where(first < limit, 1.0, 0.0) + joined * after[:, :1]
    group[tile_of(t, cap), :] = (sums / jnp.maximum(sizes, 1.0)).astype(LOW)
    gather_start(0, group_view)
    gather_start(2, grad_views[1])
    gather_relay(0, group_view)
    for copy in up_copies:
        copy.wait()
    gather_finish(0, group_view)

    def up_step(j, carry):
        wide[t, :, tile_of(j, tile)] = dot(group[...], w_up[:, tile_of(j, tile)]).astype(LOW)
        gather_start(3 + j, wide_view(j))
        return carry

    lax.fori_loop(0, tiles, up_step, 0)

    far_half = 1 - mine // (seq_size // 2)

    def send_heads(a, j, block):
        for u in range(2):
            h = 2 * j + u
            part = block[:, u * HEAD_DIM : (u + 1) * HEAD_DIM]

            @pl.when(h == mine)
            def _():
                heads[a, own_rows, :] = part

            @pl.when(h != mine)
            def _():
                outbox[a, h] = part
                remote(
                    outbox.at[a, h],
                    heads.at[a, own_rows],
                    out_send.at[a, h],
                    out_recv.at[a, mine],
                    {"seq": h},
                ).start()

    def tile_order(jj):
        return lax.rem(far_half * (tiles // 2) + jj, tiles)

    for p in range(2):
        gather_relay(1 + p, grad_views[p])
    for copy in out_copies:
        copy.wait()
    for p in range(2):
        gather_finish(1 + p, grad_views[p])

    def d_attn_step(jj, carry):
        j = tile_order(jj)
        acc = jnp.zeros((rows, tile), WIDE)
        for q in range(tp_size):
            acc += dot_last(
                wide_grad[q], w_out[tile_of(j, tile), q * columns : (q + 1) * columns]
            )
        send_heads(3, j, acc.astype(LOW))
        return carry

    lax.fori_loop(0, tiles, d_attn_step, 0)

    def relay_step(j, carry):
        gather_relay(3 + j, wide_view(j))
        return carry

    def finish_step(j, carry):
        gather_finish(3 + j, wide_view(j))
        return carry

    lax.fori_loop(0, tiles, relay_step, 0)
    lax.fori_loop(0, tiles, finish_step, 0)

    def norm_step(q, square):
        piece = wide[q].astype(WIDE)
        scaled[q] = (piece * gain[:, tile_of(q, columns)]).astype(LOW)
        return square + jnp.sum(piece * piece, 1, keepdims=True)

    square = lax.fori_loop(0, tp_size, norm_step, jnp.zeros((rows, 1), WIDE))
    rinv_column[...] = lax.rsqrt(square / model_width + EPS)

    def project(a, weight, copies):
        for copy in copies:
            copy.wait()

        def step(jj, carry):
            j = tile_order(jj)
            acc = jnp.zeros((rows, tile), WIDE)
            for q in range(tp_size):
                acc += dot(scaled[q], weight[q * columns : (q + 1) * columns, tile_of(j, tile)])
            send_heads(a, j, (rinv_column[...] * acc).astype(LOW))
            return carry

        lax.fori_loop(0, tiles, step, 0)

    project(1, w_key, key_copies)
    project(0, w_query, query_copies)
    project(2, w_value, value_copies)

    def heads_arrived(a):
        for offset in range(1, seq_size):
            source = lax.rem(mine + offset, seq_size)
            place = heads.at[a, tile_of(source, rows)]
            remote(
                place, place, out_send.at[a, source], out_recv.at[a, source], {"seq": source}
            ).wait_recv()

    for a in (3, 1, 0, 2):
        heads_arrived(a)

    blocks = patches_total // tile

    def turn_step(j, carry):
        at = tile_of(j, tile)
        key_turned[:, at] = heads[1, at, :].astype(WIDE).T.astype(LOW)
        value_turned[:, at] = heads[2, at, :].astype(WIDE).T.astype(LOW)
        key_sum[at, :] = jnp.zeros((tile, HEAD_DIM), WIDE)
        value_sum[at, :] = jnp.zeros((tile, HEAD_DIM), WIDE)
        return carry

    lax.fori_loop(0, blocks, turn_step, 0)

    def attend(i):
        queries = pl.ds(i * tile, tile)

        def score_step(j, peak):
            at = tile_of(j, tile)
            score = dot_last(heads[1, at, :], heads[0, queries, :]) * scale
            key = lax.broadcasted_iota(jnp.int32, (tile, tile), 0) + j * tile
            query = lax.broadcasted_iota(jnp.int32, (tile, tile), 1) + i * tile
            score = jnp.where((valid_column[at, :] > 0.5) & (key <= query), score, NEG)
            scores[at, :] = score
            d_probs[at, :] = dot_last(heads[2, at, :], heads[3, queries, :])
            return jnp.maximum(peak, jnp.max(score, 0, keepdims=True))

        peak = lax.fori_loop(0, i + 1, score_step, jnp.full((1, tile), NEG, WIDE))

        def mix_step(j, carry):
            total, mixed = carry
            at = tile_of(j, tile)
            expo = jnp.exp(scores[at, :] - peak)
            scores[at, :] = expo
            total += jnp.sum(expo, 0, keepdims=True)
            mixed += dot(value_turned[:, at], expo.astype(LOW))
            return total, mixed

        total, mixed = lax.fori_loop(
            0,
            i + 1,
            mix_step,
            (jnp.zeros((1, tile), WIDE), jnp.zeros((HEAD_DIM, tile), WIDE)),
        )
        share = 1.0 / total
        attn = (mixed / total).astype(LOW).astype(WIDE)
        delta = jnp.sum(heads[3, queries, :].astype(WIDE).T * attn, 0, keepdims=True)
        returns[0, queries, :] = attn.T.astype(LOW)

        def grad_step(j, query_sum):
            at = tile_of(j, tile)
            probs = scores[at, :] * share
            d_scores = (probs * (d_probs[at, :] - delta)).astype(LOW)
            value_sum[at, :] += dot(probs.astype(LOW), heads[3, queries, :])
            key_sum[at, :] += dot(d_scores, heads[0, queries, :])
            return query_sum + dot(key_turned[:, at], d_scores)

        query_sum = lax.fori_loop(0, i + 1, grad_step, jnp.zeros((HEAD_DIM, tile), WIDE))
        returns[1, queries, :] = (query_sum * scale).T.astype(LOW)
        returns[2, queries, :] = value_sum[queries, :].astype(LOW)
        returns[3, queries, :] = (key_sum[queries, :] * scale).astype(LOW)

    own_columns = tile_of(mine, HEAD_DIM)

    def return_copy(a, peer):
        return remote(
            returns.at[a, pl.ds(peer * rows, rows)],
            back.at[a, :, own_columns],
            back_send.at[a, peer],
            back_recv.at[a, mine],
            {"seq": peer},
        )

    returned = returns.shape[0]
    for i in reversed(range(blocks)):
        attend(i)
        for a in range(returned):
            for peer in range(i * tile // rows, (i + 1) * tile // rows):

                @pl.when(peer != mine)
                def _():
                    return_copy(a, peer).start()

                @pl.when(peer == mine)
                def _():
                    back[a, :, own_columns] = returns[a, peer * rows : (peer + 1) * rows, :]

    def returns_arrived(a):
        for offset in range(1, seq_size):
            source = lax.rem(mine + offset, seq_size)
            place = back.at[a, :, tile_of(source, HEAD_DIM)]
            remote(
                place, place, back_send.at[a, source], back_recv.at[a, source], {"seq": source}
            ).wait_recv()

    order = (
        (1 - chip) * 2 + (1 - core),
        (1 - chip) * 2 + core,
        chip * 2 + (1 - core),
        chip * 2 + core,
    )

    def pair_copy(a, k):
        return remote(
            partial.at[a, order[2 * k]],
            pair_in.at[a, k],
            pair_send.at[a, k],
            pair_recv.at[a, k],
            {"tp": partner},
        )

    def cross_copy(a):
        return remote(
            cross_out.at[a], cross_in.at[a], cross_send.at[a], cross_recv.at[a], {"tp": across}
        )

    returns_arrived(0)
    for k in range(tp_size):
        quarter = order[k]

        def value_step(j, carry):
            at = tile_of(quarter * tiles + j, tile)
            partial[0, quarter, :, tile_of(j, tile)] = dot(back[0], w_out[:, at]).astype(LOW)
            return carry

        lax.fori_loop(0, tiles, value_step, 0)
        if k % 2 == 0:
            pair_copy(0, k // 2).start()
    pair_copy(0, 0).wait_recv()
    cross_out[0] = (partial[0, order[1]].astype(WIDE) + pair_in[0, 0].astype(WIDE)).astype(LOW)
    cross_copy(0).start()

    for a, weight in ((1, w_query), (2, w_value)):
        returns_arrived(a)
        for quarter in range(tp_size):

            def grad_in_step(j, carry):
                at = tile_of(quarter * tiles + j, tile)
                more = dot_last(back[a], weight[at, :])
                here = tile_of(j, tile)
                if a == 1:
                    grad_sum[quarter, :, here] = more
                else:
                    grad_sum[quarter, :, here] += more
                return carry

            lax.fori_loop(0, tiles, grad_in_step, 0)
    returns_arrived(3)
    dots = jnp.zeros((rows, 1), WIDE)
    for k in range(tp_size):
        quarter = order[k]

        def last_step(j, dots):
            at = tile_of(quarter * tiles + j, tile)
            here = tile_of(j, tile)
            whole = grad_sum[quarter, :, here] + dot_last(back[3], w_key[at, :])
            partial[1, quarter, :, here] = whole.astype(LOW)
            inner = gain[:, at] * whole * wide[quarter, :, here].astype(WIDE)
            return dots + jnp.sum(inner, 1, keepdims=True)

        dots = lax.fori_loop(0, tiles, last_step, dots)
        if k % 2 == 0:
            pair_copy(1, k // 2).start()
        if k == 1:
            pair_copy(1, 0).wait_recv()
            cross_out[1] = (
                partial[1, order[1]].astype(WIDE) + pair_in[1, 0].astype(WIDE)
            ).astype(LOW)
            cross_copy(1).start()

    def dots_copy(offset):
        return remote(
            dots_out,
            dots_in.at[offset],
            dots_send.at[offset],
            dots_recv.at[offset],
            {"tp": lax.rem(t + offset, tp_size)},
        )

    dots_out[...] = jnp.broadcast_to(to_row(dots), dots_out.shape)
    for offset in range(1, tp_size):
        dots_copy(offset).start()

    wide_in = wide[t].astype(WIDE)
    rinv = rinv_column[...]
    pair_copy(0, 1).wait_recv()
    cross_copy(0).wait_recv()
    total_value = (
        partial[0, t].astype(WIDE) + pair_in[0, 1].astype(WIDE) + cross_in[0].astype(WIDE)
    )
    out_value[...] = jnp.where(row_valid > 0.5, wide_in + total_value, 0.0).astype(LOW)
    for offset in range(1, tp_size):
        dots_copy(offset).wait_recv()
        dots += to_column(dots_in[offset][:1])
    pair_copy(1, 1).wait_recv()
    cross_copy(1).wait_recv()
    total_grad = (
        partial[1, t].astype(WIDE) + pair_in[1, 1].astype(WIDE) + cross_in[1].astype(WIDE)
    )
    out_grad[...] = (
        wide_grad[t].astype(WIDE)
        + rinv * gain[:, tile_of(t, columns)] * total_grad
        - wide_in * (rinv**3 * dots / model_width)
    )

    @pl.when(has_before)
    def _():
        lead_copy.wait_send()

    gather_drain(0, group_view)
    for p in range(2):
        gather_drain(1 + p, grad_views[p])

    def drain_step(j, carry):
        gather_drain(3 + j, wide_view(j))
        return carry

    lax.fori_loop(0, tiles, drain_step, 0)
    for offset in range(1, seq_size):
        peer = lax.rem(mine + offset, seq_size)
        for a in range(heads.shape[0]):
            remote(
                outbox.at[a, peer],
                heads.at[a, own_rows],
                out_send.at[a, peer],
                out_recv.at[a, mine],
                {"seq": peer},
            ).wait_send()
        for a in range(returned):
            remote(
                returns.at[a, tile_of(peer, rows)],
                back.at[a, :, own_columns],
                back_send.at[a, peer],
                back_recv.at[a, mine],
                {"seq": peer},
            ).wait_send()
    for a in range(2):
        for k in range(2):
            pair_copy(a, k).wait_send()
        cross_copy(a).wait_send()
    for offset in range(1, tp_size):
        dots_copy(offset).wait_send()


def per_device_whole(encoded, starts, w_up, norm_gain, w_query, w_key, w_value, w_out, cotangent):
    seq_size, tp_size = lax.axis_size("seq"), lax.axis_size("tp")
    rows, columns = cotangent.shape
    model_width = norm_gain.shape[0]
    byte_width = encoded.shape[1]
    cap = starts.shape[1]
    total = starts.size
    tile = 2 * HEAD_DIM
    chunks = 3 + columns // tile
    dma = pltpu.SemaphoreType.DMA
    scratch = [
        pltpu.VMEM(w_up.shape, LOW),
        pltpu.VMEM(w_query.shape, LOW),
        pltpu.VMEM(w_key.shape, LOW),
        pltpu.VMEM(w_value.shape, LOW),
        pltpu.VMEM(w_out.shape, LOW),
        pltpu.VMEM((1, byte_width), WIDE),
        pltpu.VMEM((1, byte_width), WIDE),
        pltpu.VMEM((rows, byte_width), LOW),
        pltpu.VMEM((tp_size, rows, columns), LOW),
        pltpu.VMEM((tp_size, rows, columns), LOW),
        pltpu.VMEM((tp_size, rows, columns), LOW),
        pltpu.VMEM((total, 1), WIDE),
        pltpu.VMEM((rows, 1), WIDE),
        pltpu.VMEM((4, seq_size, rows, HEAD_DIM), LOW),
        pltpu.VMEM((4, total, HEAD_DIM), LOW),
        pltpu.VMEM((HEAD_DIM, total), LOW),
        pltpu.VMEM((HEAD_DIM, total), LOW),
        pltpu.VMEM((total, tile), WIDE),
        pltpu.VMEM((total, tile), WIDE),
        pltpu.VMEM((total, HEAD_DIM), WIDE),
        pltpu.VMEM((total, HEAD_DIM), WIDE),
        pltpu.VMEM((4, total, HEAD_DIM), LOW),
        pltpu.VMEM((4, rows, columns), LOW),
        pltpu.VMEM((tp_size, rows, columns), WIDE),
        pltpu.VMEM((2, tp_size, rows, columns), LOW),
        pltpu.VMEM((2, 2, rows, columns), LOW),
        pltpu.VMEM((2, rows, columns), LOW),
        pltpu.VMEM((2, rows, columns), LOW),
        pltpu.VMEM((8, rows), WIDE),
        pltpu.VMEM((tp_size, 8, rows), WIDE),
        dma((5, 4)),
        dma((2,)),
        dma((3, chunks)),
        dma((3, chunks)),
        dma((4, seq_size)),
        dma((4, seq_size)),
        dma((4, seq_size)),
        dma((4, seq_size)),
            dma((2, 2)),
        dma((2, 2)),
        dma((2,)),
        dma((2,)),
        dma((tp_size,)),
        dma((tp_size,)),
    ]
    near = pl.BlockSpec(memory_space=pltpu.VMEM)
    far = pl.BlockSpec(memory_space=pl.ANY)
    return tuple(
        pl.pallas_call(
            functools.partial(layer_kernel, seq_size, tp_size),
            out_shape=[
                jax.ShapeDtypeStruct((rows, columns), LOW),
                jax.ShapeDtypeStruct((rows, columns), WIDE),
            ],
            in_specs=[near] * 4 + [far] * 5,
            out_specs=[near] * 2,
            scratch_shapes=scratch,
            compiler_params=pltpu.CompilerParams(
                collective_id=0, has_side_effects=True, vmem_limit_bytes=67043328
            ),
        )(
            encoded,
            starts,
            norm_gain.reshape(1, model_width),
            cotangent,
            w_up,
            w_query,
            w_key,
            w_value,
            w_out,
        )
    )


def fits_one_kernel(arrays):
    encoded, starts, w_up, norm_gain, w_query, w_key, w_value, w_out, cotangent = arrays
    seq_size, tp_size = lax.axis_size("seq"), lax.axis_size("tp")
    rows, columns = cotangent.shape
    cap = starts.shape[1]
    return (
        tp_size == 4
        and seq_size % 2 == 0
        and columns == seq_size * HEAD_DIM
        and rows == HEAD_DIM
        and rows == tp_size * cap
        and cap & (cap - 1) == 0
        and cap % 16 == 0
        and columns % (4 * HEAD_DIM) == 0
        and norm_gain.shape[0] == tp_size * columns
        and starts.shape[0] == seq_size * tp_size
        and starts.size % (2 * HEAD_DIM) == 0
    )


def solution(mesh):
    in_specs = (
        P(("seq", "tp"), None),
        P(),
        P(None, "tp"),
        P(),
        P(None, "tp"),
        P(None, "tp"),
        P(None, "tp"),
        P("tp", None),
        P("seq", "tp"),
    )
    out_specs = (P("seq", "tp"), P("seq", "tp"))

    def choose(*arrays):
        return (per_device_whole if fits_one_kernel(arrays) else per_device)(*arrays)

    return jax.shard_map(
        choose, mesh=mesh, in_specs=in_specs, out_specs=out_specs, check_vma=False
    )
```

time: 191 us -> 104 us (0.54)
  matrix products: 53.3 us -> 0 us
  Pallas kernels: 117 us -> 99.4 us
  other arithmetic: 13.2 us -> 0 us
  starting transfers between devices: 2.58 us -> 0 us
    dot_general x17 -> x0, matrix products: 53.3 us -> none  [the longest x3 9.79 us: project(): acc = jnp.dot(scaled, weight, preferred_element_type=jnp.float32)]
    pallas_call x5 -> x1, Pallas kernels: 117 us -> 99.4 us  [per_device_whole(): pl.pallas_call(functools.partial(layer_kernel, seq_size, tp_size), out_sh...]
    reduce_sum x7 -> x0, other arithmetic: 8.77 us -> none  [the longest x1 2.06 us: add_up(): jnp.sum(parts.reshape(-1, group_rows, columns).astype(jnp.float32), 0)]
    ppermute x2 -> x0, starting transfers between devices: 2.58 us -> none  [shifted(): return lax.ppermute(block, axis, route)]
    unnamed x44 -> x2, local copies, waits for them, and re-layouts: 1.3 us -> 3.55 us
  transfers between devices with their start and end apart: 2 -> 0, of which waited for: 0 -> 0; matrix products, arithmetic and copies ran while one was open for 3% -> 0% of each run, Pallas kernels for 0% -> 0%
where the time goes in v1:
time: 104 us
  Pallas kernels  99.4 us (96%)
  local copies, waits for them, and re-layouts  3.55 us (3%)
    pallas_call x1, Pallas kernels, per_device_whole(): pl.pallas_call(functools.partial(layer_kernel, seq_size, tp_size), out_sh...  99.4 us
    unnamed x2, local copies, waits for them, and re-layouts  3.55 us

profile of v1, /device:TPU:0, one launch (start us, length us, event | category | flops | bytes accessed | tf_op | source)
XLA Modules:
  0.0 103.6 jit_solution(7305041504546600023)
XLA Ops:
  0.6 99.4 %shard_map.104 = (bf16[128,1024]{1,0:T(8,128)(2,1)}, f32[128,1024]{1,0:T(8,128)}) custom-call(bf16[256,1280]{1,0:T(8,128)(2,1)} %encoded.1, s32[32,32]{1,0:T(8,128)} %starts.1, f32[1,4096]{1,0:T(1,128)} %bitcast.1, bf16[128,1024]{1,0:T(8,128)(2,1)} %cotangent.1, bf16[1280,1024]{1,0:T(8,128)(2,1)} %w_up_far.1, bf16[4096,1024]{1,0:T(8,128)(2,1)} %w_query_far.1, ...), custom_call_target="tpu_custom_call" | custom-call | tf_op jit(solution)/shard_map/pallas_call | solution.py:816
  100.1 1.7 %copy.13 = bf16[128,1024]{1,0:T(8,128)(2,1)} copy(bf16[128,1024]{1,0:T(8,128)(2,1)} %get-tuple-element.4) | data formatting | bytes 524288
  101.7 1.9 %copy.14 = f32[128,1024]{1,0:T(8,128)} copy(f32[128,1024]{1,0:T(8,128)} %get-tuple-element.5) | data formatting | bytes 1048576

commit v2 on v1

--- a/solution.py
+++ b/solution.py
@@ -168,27 +168,27 @@
     return lax.dot_general(a, b, CONTRACT_LAST, preferred_element_type=WIDE)
 
 
-def to_row(column):
+def to_row(column, lanes):
     n = column.shape[0]
-    down = lax.broadcasted_iota(jnp.int32, (n, n), 0)
-    across = lax.broadcasted_iota(jnp.int32, (n, n), 1)
+    down = lax.broadcasted_iota(jnp.int32, (n, lanes), 0)
+    across = lax.broadcasted_iota(jnp.int32, (n, lanes), 1)
     return jnp.sum(jnp.where(down == across, column, 0.0), 0, keepdims=True)
 
 
-def to_column(row, shift=0):
-    n = row.shape[1]
-    down = lax.broadcasted_iota(jnp.int32, (n, n), 0)
-    across = lax.broadcasted_iota(jnp.int32, (n, n), 1)
+def to_column(row, n, shift=0):
+    lanes = row.shape[1]
+    down = lax.broadcasted_iota(jnp.int32, (n, lanes), 0)
+    across = lax.broadcasted_iota(jnp.int32, (n, lanes), 1)
     return jnp.sum(jnp.where(down + shift == across, row, 0.0), 1, keepdims=True)
 
 
 def layer_kernel(
     seq_size,
     tp_size,
-    encoded,
-    starts,
-    gain,
-    cotangent,
+    starts_far,
+    gain_far,
+    encoded_far,
+    cotangent_far,
     w_up_far,
     w_query_far,
     w_key_far,
@@ -196,6 +196,10 @@
     w_out_far,
     out_value,
     out_grad,
+    starts,
+    gain,
+    encoded,
+    cotangent,
     w_up,
     w_query,
     w_key,
@@ -208,13 +212,15 @@
     wide_grad,
     scaled,
     valid_column,
+    key_bias,
     rinv_column,
     outbox,
     heads,
     value_turned,
     key_turned,
     scores,
-    d_probs,
+    attn_turned,
+    share_row,
     key_sum,
     value_sum,
     returns,
@@ -227,6 +233,7 @@
     dots_out,
     dots_in,
     weight_sem,
+    near_sem,
     lead_sem,
     gather_send,
     gather_recv,
@@ -267,26 +274,6 @@
             device_id_type=MESH,
         )
 
-    pieces = weight_sem.shape[1]
-
-    def weight_copies(i, far, near):
-        depth = far.shape[0] // pieces
-        return [
-            pltpu.make_async_copy(
-                far.at[pl.ds(p * depth, depth)], near.at[pl.ds(p * depth, depth)], weight_sem.at[i, p]
-            )
-            for p in range(pieces)
-        ]
-
-    up_copies = weight_copies(0, w_up_far, w_up)
-    out_copies = weight_copies(1, w_out_far, w_out)
-    key_copies = weight_copies(2, w_key_far, w_key)
-    query_copies = weight_copies(3, w_query_far, w_query)
-    value_copies = weight_copies(4, w_value_far, w_value)
-    for copies in (up_copies, out_copies, key_copies, query_copies, value_copies):
-        for copy in copies:
-            copy.start()
-
     barrier = pltpu.get_barrier_semaphore()
     for offset in range(1, tp_size):
         pl.semaphore_signal(
@@ -317,17 +304,46 @@
     def _():
         pl.semaphore_signal(barrier, inc=1, device_id=shard_after, device_id_type=MESH)
 
+    near_copies = [
+        pltpu.make_async_copy(starts_far, starts, near_sem.at[0]),
+        pltpu.make_async_copy(encoded_far, encoded, near_sem.at[1]),
+        pltpu.make_async_copy(cotangent_far, cotangent, near_sem.at[2]),
+        pltpu.make_async_copy(gain_far, gain, near_sem.at[3]),
+    ]
+    for copy in near_copies:
+        copy.start()
+    pieces = weight_sem.shape[1]
+
+    def weight_copies(i, far, near):
+        depth = far.shape[0] // pieces
+        return [
+            pltpu.make_async_copy(
+                far.at[pl.ds(p * depth, depth)], near.at[pl.ds(p * depth, depth)], weight_sem.at[i, p]
+            )
+            for p in range(pieces)
+        ]
+
+    up_copies = weight_copies(0, w_up_far, w_up)
+    out_copies = weight_copies(1, w_out_far, w_out)
+    key_copies = weight_copies(2, w_key_far, w_key)
+    query_copies = weight_copies(3, w_query_far, w_query)
+    value_copies = weight_copies(4, w_value_far, w_value)
+    near_copies[0].wait()
     limit = float(byte_rows)
     own = starts[pl.ds(shard, 1), :].astype(WIDE)
     after = starts[pl.ds(jnp.minimum(shard + 1, shards - 1), 1), :].astype(WIDE)
-    first = to_column(own)
+    first = to_column(own, cap)
     slot = lax.broadcasted_iota(jnp.int32, (cap, 1), 0)
-    following = to_column(own, 1) + jnp.where(slot == cap - 1, limit, 0.0)
+    following = to_column(own, cap, 1) + jnp.where(slot == cap - 1, limit, 0.0)
     places = lax.broadcasted_iota(jnp.int32, (cap, byte_rows), 1).astype(WIDE)
     inside = jnp.where((places >= first) & (places < following), 1.0, 0.0).astype(LOW)
     lead_places = lax.broadcasted_iota(jnp.int32, (16, byte_rows), 1).astype(WIDE)
     leading = jnp.where(lead_places < own[:, :1], 1.0, 0.0).astype(LOW)
+    near_copies[1].wait()
+    for copy in up_copies:
+        copy.start()
     lead_out[...] = dot(leading, encoded[...])[:1]
+    sums = dot(inside, encoded[...])
 
     index = lax.broadcasted_iota(jnp.int32, (patches_total, shards), 0)
     lane = lax.broadcasted_iota(jnp.int32, (patches_total, shards), 1)
@@ -341,8 +357,10 @@
     )
     own_rows = tile_of(mine, rows)
     row_valid = valid_column[own_rows, :]
+    key_bias[...] = jnp.broadcast_to((valid_column[...] - 1.0) * -NEG, key_bias.shape)
+    near_copies[2].wait()
     wide_grad[t] = jnp.where(row_valid > 0.5, cotangent[...].astype(WIDE), 0.0).astype(LOW)
-    sums = dot(inside, encoded[...])
+    near_copies[3].wait()
 
     neighbours = group_first.astype(jnp.int32) + group_last.astype(jnp.int32)
     pl.semaphore_wait(barrier, tp_size + seq_size - 2 + neighbours)
@@ -371,9 +389,9 @@
             piece, piece, gather_send.at[2, k], gather_recv.at[2, k], {"tp": partner}
         ).start()
 
-    def gather_finish(k, view):
-        for way, origin in ((1, partner), (2, diagonal)):
-            piece = view(origin)
+    def gather_finish(k, view, ways=(1, 2)):
+        for way in ways:
+            piece = view(partner if way == 1 else diagonal)
             remote(
                 piece, piece, gather_send.at[way, k], gather_recv.at[way, k], {"tp": partner}
             ).wait_recv()
@@ -385,16 +403,28 @@
                 piece, piece, gather_send.at[way, k], gather_recv.at[way, k], {"tp": target}
             ).wait_send()
 
-    half_rows = rows // 2
+    grad_pieces = 4
+    piece_rows = rows // grad_pieces
     grad_views = [
-        lambda q, p=p: wide_grad.at[q, pl.ds(p * half_rows, half_rows)] for p in range(2)
+        lambda q, p=p: wide_grad.at[q, pl.ds(p * piece_rows, piece_rows)]
+        for p in range(grad_pieces)
     ]
     group_view = lambda q: group.at[tile_of(q, cap)]
-
-    def wide_view(j):
-        return lambda q: wide.at[q, :, tile_of(j, tile)]
-
-    gather_start(1, grad_views[0])
+    half_rows = rows // 2
+    wide_tile = columns // 2
+
+    def wide_view(batch, j):
+        def view(q):
+            of_chip = q // 2
+            place = of_chip if batch == 0 else 1 - of_chip
+            return wide.at[
+                q, tile_of(place, half_rows), j * wide_tile : (j + 1) * wide_tile
+            ]
+
+        return view
+
+    def wide_chunk(batch, j):
+        return 1 + grad_pieces + 2 * batch + j
 
     @pl.when(has_after)
     def _():
@@ -407,49 +437,127 @@
     sizes = (following - first) * jnp.where(first < limit, 1.0, 0.0) + joined * after[:, :1]
     group[tile_of(t, cap), :] = (sums / jnp.maximum(sizes, 1.0)).astype(LOW)
     gather_start(0, group_view)
-    gather_start(2, grad_views[1])
-    gather_relay(0, group_view)
+    for copies in (key_copies, query_copies, value_copies, out_copies):
+        for copy in copies:
+            copy.start()
+
+    def raise_rows(batch):
+        place = tile_of(chip if batch == 0 else 1 - chip, half_rows)
+        for j in range(2):
+            cut = slice(j * wide_tile, (j + 1) * wide_tile)
+            wide[t, place, cut] = dot(group[place, :], w_up[:, cut]).astype(LOW)
+            gather_start(wide_chunk(batch, j), wide_view(batch, j))
+
+    gather_finish(0, group_view, (1,))
     for copy in up_copies:
         copy.wait()
-    gather_finish(0, group_view)
-
-    def up_step(j, carry):
-        wide[t, :, tile_of(j, tile)] = dot(group[...], w_up[:, tile_of(j, tile)]).astype(LOW)
-        gather_start(3 + j, wide_view(j))
-        return carry
-
-    lax.fori_loop(0, tiles, up_step, 0)
+    raise_rows(0)
+    gather_relay(0, group_view)
+    gather_finish(0, group_view, (2,))
+    raise_rows(1)
 
     far_half = 1 - mine // (seq_size // 2)
 
-    def send_heads(a, j, block):
+    def head_copy(k, h):
+        if k == 6:
+            src, place = outbox.at[3, h], own_rows
+        else:
+            a, batch = k // 2, k % 2
+            piece = 1 - chip if batch == 0 else chip
+            src = outbox.at[a, h, tile_of(piece, half_rows)]
+            place = tile_of(2 * mine + piece, half_rows)
+        return remote(
+            src,
+            heads.at[3 if k == 6 else k // 2, place],
+            out_send.at[k, h],
+            out_recv.at[k, mine],
+            {"seq": h},
+        )
+
+    def start_head(k, h):
+        @pl.when(h != mine)
+        def _():
+            head_copy(k, h).start()
+
+    def keep_heads(a, j, block, start, size):
         for u in range(2):
             h = 2 * j + u
             part = block[:, u * HEAD_DIM : (u + 1) * HEAD_DIM]
 
             @pl.when(h == mine)
             def _():
-                heads[a, own_rows, :] = part
+                heads[a, pl.ds(pl.multiple_of(mine * rows + start, size), size), :] = part
 
             @pl.when(h != mine)
             def _():
-                outbox[a, h] = part
-                remote(
-                    outbox.at[a, h],
-                    heads.at[a, own_rows],
-                    out_send.at[a, h],
-                    out_recv.at[a, mine],
-                    {"seq": h},
-                ).start()
+                outbox[a, h, pl.ds(pl.multiple_of(start, size), size), :] = part
 
     def tile_order(jj):
         return lax.rem(far_half * (tiles // 2) + jj, tiles)
 
-    for p in range(2):
+    def relay_rows(batch):
+        for j in range(2):
+            gather_relay(wide_chunk(batch, j), wide_view(batch, j))
+
+    def norm_rows(batch):
+        place = tile_of(1 - chip if batch == 0 else chip, half_rows)
+
+        def norm_step(q, square):
+            piece = wide[q, place].astype(WIDE)
+            scaled[q, place] = (piece * gain[:, tile_of(q, columns)]).astype(LOW)
+            return square + jnp.sum(piece * piece, 1, keepdims=True)
+
+        square = lax.fori_loop(0, tp_size, norm_step, jnp.zeros((half_rows, 1), WIDE))
+        rinv_column[place, :] = lax.rsqrt(square / model_width + EPS)
+
+    def project(a, weight, batch):
+        piece = 1 - chip if batch == 0 else chip
+        place = tile_of(piece, half_rows)
+
+        def step(jj, carry):
+            j = tile_order(jj)
+            acc = jnp.zeros((half_rows, tile), WIDE)
+            for q in range(tp_size):
+                acc += dot(
+                    scaled[q, place], weight[q * columns : (q + 1) * columns, tile_of(j, tile)]
+                )
+            block = (rinv_column[place, :] * acc).astype(LOW)
+            keep_heads(a, j, block, piece * half_rows, half_rows)
+            for u in range(2):
+                start_head(2 * a + batch, 2 * j + u)
+            return carry
+
+        lax.fori_loop(0, tiles, step, 0)
+
+    relay_rows(0)
+    for j in range(2):
+        gather_finish(wide_chunk(0, j), wide_view(0, j), (2,))
+        gather_finish(wide_chunk(1, j), wide_view(1, j), (1,))
+    norm_rows(0)
+    for copy in key_copies:
+        copy.wait()
+    project(1, w_key, 0)
+    relay_rows(1)
+    for p in range(grad_pieces):
+        gather_start(1 + p, grad_views[p])
+    for copy in query_copies:
+        copy.wait()
+    project(0, w_query, 0)
+    for copy in value_copies:
+        copy.wait()
+    project(2, w_value, 0)
+    for j in range(2):
+        gather_finish(wide_chunk(0, j), wide_view(0, j), (1,))
+        gather_finish(wide_chunk(1, j), wide_view(1, j), (2,))
+    norm_rows(1)
+    project(1, w_key, 1)
+    project(0, w_query, 1)
+    for p in range(grad_pieces):
         gather_relay(1 + p, grad_views[p])
+    project(2, w_value, 1)
     for copy in out_copies:
         copy.wait()
-    for p in range(2):
+    for p in range(grad_pieces):
         gather_finish(1 + p, grad_views[p])
 
     def d_attn_step(jj, carry):
@@ -459,150 +567,144 @@
             acc += dot_last(
                 wide_grad[q], w_out[tile_of(j, tile), q * columns : (q + 1) * columns]
             )
-        send_heads(3, j, acc.astype(LOW))
+        keep_heads(3, j, acc.astype(LOW), 0, rows)
         return carry
 
     lax.fori_loop(0, tiles, d_attn_step, 0)
 
-    def relay_step(j, carry):
-        gather_relay(3 + j, wide_view(j))
-        return carry
-
-    def finish_step(j, carry):
-        gather_finish(3 + j, wide_view(j))
-        return carry
-
-    lax.fori_loop(0, tiles, relay_step, 0)
-    lax.fori_loop(0, tiles, finish_step, 0)
-
-    def norm_step(q, square):
-        piece = wide[q].astype(WIDE)
-        scaled[q] = (piece * gain[:, tile_of(q, columns)]).astype(LOW)
-        return square + jnp.sum(piece * piece, 1, keepdims=True)
-
-    square = lax.fori_loop(0, tp_size, norm_step, jnp.zeros((rows, 1), WIDE))
-    rinv_column[...] = lax.rsqrt(square / model_width + EPS)
-
-    def project(a, weight, copies):
-        for copy in copies:
-            copy.wait()
-
-        def step(jj, carry):
-            j = tile_order(jj)
-            acc = jnp.zeros((rows, tile), WIDE)
-            for q in range(tp_size):
-                acc += dot(scaled[q], weight[q * columns : (q + 1) * columns, tile_of(j, tile)])
-            send_heads(a, j, (rinv_column[...] * acc).astype(LOW))
-            return carry
-
-        lax.fori_loop(0, tiles, step, 0)
-
-    project(1, w_key, key_copies)
-    project(0, w_query, query_copies)
-    project(2, w_value, value_copies)
-
-    def heads_arrived(a):
+
+    def heads_arrived(k):
         for offset in range(1, seq_size):
             source = lax.rem(mine + offset, seq_size)
-            place = heads.at[a, tile_of(source, rows)]
+            if k == 6:
+                place = heads.at[3, tile_of(source, rows)]
+            else:
+                piece = 1 - chip if k % 2 == 0 else chip
+                place = heads.at[k // 2, tile_of(2 * source + piece, half_rows)]
             remote(
-                place, place, out_send.at[a, source], out_recv.at[a, source], {"seq": source}
+                place, place, out_send.at[k, source], out_recv.at[k, source], {"seq": source}
             ).wait_recv()
 
-    for a in (3, 1, 0, 2):
-        heads_arrived(a)
+    for k in (2, 0, 4, 3, 1):
+        heads_arrived(k)
+    for step in range(seq_size):
+        start_head(6, lax.rem(far_half * (seq_size // 2) + step, seq_size))
+    heads_arrived(5)
 
     blocks = patches_total // tile
-
-    def turn_step(j, carry):
-        at = tile_of(j, tile)
-        key_turned[:, at] = heads[1, at, :].astype(WIDE).T.astype(LOW)
-        value_turned[:, at] = heads[2, at, :].astype(WIDE).T.astype(LOW)
-        key_sum[at, :] = jnp.zeros((tile, HEAD_DIM), WIDE)
-        value_sum[at, :] = jnp.zeros((tile, HEAD_DIM), WIDE)
-        return carry
-
-    lax.fori_loop(0, blocks, turn_step, 0)
+    own_columns = tile_of(mine, HEAD_DIM)
+
+    def piece_of(k):
+        if k < 3:
+            return k, 0, rows
+        return 3, half_rows * (k - 3), half_rows
+
+    def return_copy(k, peer):
+        a, start, size = piece_of(k)
+        return remote(
+            returns.at[a, pl.ds(peer * rows + start, size)],
+            back.at[a, start : start + size, own_columns],
+            back_send.at[k, peer],
+            back_recv.at[k, mine],
+            {"seq": peer},
+        )
+
+    def send_back(k, i):
+        a, start, size = piece_of(k)
+        for peer in range(i * tile // rows, (i + 1) * tile // rows):
+
+            @pl.when(peer != mine)
+            def _():
+                return_copy(k, peer).start()
+
+            @pl.when(peer == mine)
+            def _():
+                first = peer * rows + start
+                back[a, start : start + size, own_columns] = returns[a, first : first + size, :]
+
+    def sent_back(k):
+        for peer in range(seq_size):
+
+            @pl.when(peer != mine)
+            def _():
+                return_copy(k, peer).wait_send()
+
+    def cut_of(i):
+        return slice(i * tile, (i + 1) * tile)
+
+    def score_cut(i, j):
+        return cut_of(i * (i + 1) // 2 + j)
+
+    for j in range(blocks):
+        key_turned[:, cut_of(j)] = heads[1, cut_of(j), :].astype(WIDE).T.astype(LOW)
+        value_turned[:, cut_of(j)] = heads[2, cut_of(j), :].astype(WIDE).T.astype(LOW)
 
     def attend(i):
-        queries = pl.ds(i * tile, tile)
-
-        def score_step(j, peak):
-            at = tile_of(j, tile)
-            score = dot_last(heads[1, at, :], heads[0, queries, :]) * scale
-            key = lax.broadcasted_iota(jnp.int32, (tile, tile), 0) + j * tile
-            query = lax.broadcasted_iota(jnp.int32, (tile, tile), 1) + i * tile
-            score = jnp.where((valid_column[at, :] > 0.5) & (key <= query), score, NEG)
-            scores[at, :] = score
-            d_probs[at, :] = dot_last(heads[2, at, :], heads[3, queries, :])
-            return jnp.maximum(peak, jnp.max(score, 0, keepdims=True))
-
-        peak = lax.fori_loop(0, i + 1, score_step, jnp.full((1, tile), NEG, WIDE))
-
-        def mix_step(j, carry):
-            total, mixed = carry
-            at = tile_of(j, tile)
-            expo = jnp.exp(scores[at, :] - peak)
-            scores[at, :] = expo
+        peak = jnp.full((1, tile), NEG, WIDE)
+        for j in range(i + 1):
+            score = dot_last(heads[1, cut_of(j), :], heads[0, cut_of(i), :]) * scale
+            bias = key_bias[cut_of(j), :]
+            score += jnp.concatenate([bias] * (tile // bias.shape[1]), 1)
+            if i == j:
+                key = lax.broadcasted_iota(jnp.int32, (tile, tile), 0)
+                query = lax.broadcasted_iota(jnp.int32, (tile, tile), 1)
+                score = jnp.where(key <= query, score, NEG)
+            scores[score_cut(i, j), :] = score
+            peak = jnp.maximum(peak, jnp.max(score, 0, keepdims=True))
+        total = jnp.zeros((1, tile), WIDE)
+        mixed = jnp.zeros((HEAD_DIM, tile), WIDE)
+        for j in range(i + 1):
+            expo = jnp.exp(scores[score_cut(i, j), :] - peak)
+            scores[score_cut(i, j), :] = expo
             total += jnp.sum(expo, 0, keepdims=True)
-            mixed += dot(value_turned[:, at], expo.astype(LOW))
-            return total, mixed
-
-        total, mixed = lax.fori_loop(
-            0,
-            i + 1,
-            mix_step,
-            (jnp.zeros((1, tile), WIDE), jnp.zeros((HEAD_DIM, tile), WIDE)),
-        )
-        share = 1.0 / total
+            mixed += dot(value_turned[:, cut_of(j)], expo.astype(LOW))
+        share_row[:, cut_of(i)] = 1.0 / total
         attn = (mixed / total).astype(LOW).astype(WIDE)
-        delta = jnp.sum(heads[3, queries, :].astype(WIDE).T * attn, 0, keepdims=True)
-        returns[0, queries, :] = attn.T.astype(LOW)
-
-        def grad_step(j, query_sum):
-            at = tile_of(j, tile)
-            probs = scores[at, :] * share
-            d_scores = (probs * (d_probs[at, :] - delta)).astype(LOW)
-            value_sum[at, :] += dot(probs.astype(LOW), heads[3, queries, :])
-            key_sum[at, :] += dot(d_scores, heads[0, queries, :])
-            return query_sum + dot(key_turned[:, at], d_scores)
-
-        query_sum = lax.fori_loop(0, i + 1, grad_step, jnp.zeros((HEAD_DIM, tile), WIDE))
-        returns[1, queries, :] = (query_sum * scale).T.astype(LOW)
-        returns[2, queries, :] = value_sum[queries, :].astype(LOW)
-        returns[3, queries, :] = (key_sum[queries, :] * scale).astype(LOW)
-
-    own_columns = tile_of(mine, HEAD_DIM)
-
-    def return_copy(a, peer):
-        return remote(
-            returns.at[a, pl.ds(peer * rows, rows)],
-            back.at[a, :, own_columns],
-            back_send.at[a, peer],
-            back_recv.at[a, mine],
-            {"seq": peer},
-        )
-
-    returned = returns.shape[0]
+        attn_turned[:, cut_of(i)] = attn
+        returns[0, cut_of(i), :] = attn.T.astype(LOW)
+
+    def attend_back(i):
+        grad = heads[3, cut_of(i), :]
+        delta = jnp.sum(grad.astype(WIDE).T * attn_turned[:, cut_of(i)], 0, keepdims=True)
+        share = share_row[:, cut_of(i)]
+        query_sum = jnp.zeros((HEAD_DIM, tile), WIDE)
+        for j in range(i + 1):
+            d_probs = dot_last(heads[2, cut_of(j), :], grad)
+            probs = scores[score_cut(i, j), :] * share
+            d_scores = (probs * (d_probs - delta)).astype(LOW)
+            value_part = dot(probs.astype(LOW), grad)
+            key_part = dot(d_scores, heads[0, cut_of(i), :])
+            query_sum += dot(key_turned[:, cut_of(j)], d_scores)
+            if i < blocks - 1:
+                value_part += value_sum[cut_of(j), :]
+                key_part += key_sum[cut_of(j), :]
+            if i == j:
+                returns[2, cut_of(j), :] = value_part.astype(LOW)
+                returns[3, cut_of(j), :] = (key_part * scale).astype(LOW)
+            else:
+                value_sum[cut_of(j), :] = value_part
+                key_sum[cut_of(j), :] = key_part
+        returns[1, cut_of(i), :] = (query_sum * scale).T.astype(LOW)
+
+    ends = [0] + list(reversed(range(1, blocks)))
+    for i in ends:
+        attend(i)
+        send_back(0, i)
+    heads_arrived(6)
     for i in reversed(range(blocks)):
-        attend(i)
-        for a in range(returned):
-            for peer in range(i * tile // rows, (i + 1) * tile // rows):
-
-                @pl.when(peer != mine)
-                def _():
-                    return_copy(a, peer).start()
-
-                @pl.when(peer == mine)
-                def _():
-                    back[a, :, own_columns] = returns[a, peer * rows : (peer + 1) * rows, :]
-
-    def returns_arrived(a):
-        for offset in range(1, seq_size):
-            source = lax.rem(mine + offset, seq_size)
-            place = back.at[a, :, tile_of(source, HEAD_DIM)]
+        attend_back(i)
+        send_back(1, i)
+    sent_back(0)
+    for i in reversed(range(blocks)):
+        send_back(2, i)
+
+    def returns_arrived(k):
+        a, start, size = piece_of(k)
+        for step in range(1, seq_size):
+            source = lax.rem(mine + step, seq_size)
+            place = back.at[a, start : start + size, tile_of(source, HEAD_DIM)]
             remote(
-                place, place, back_send.at[a, source], back_recv.at[a, source], {"seq": source}
+                place, place, back_send.at[k, source], back_recv.at[k, source], {"seq": source}
             ).wait_recv()
 
     order = (
@@ -611,19 +713,44 @@
         chip * 2 + (1 - core),
         chip * 2 + core,
     )
-
-    def pair_copy(a, k):
+    stages = ((0, slice(0, rows)), (1, slice(0, half_rows)), (1, slice(half_rows, rows)))
+
+    def pair_copy(stage, k):
+        a, part = stages[stage]
         return remote(
-            partial.at[a, order[2 * k]],
-            pair_in.at[a, k],
-            pair_send.at[a, k],
-            pair_recv.at[a, k],
+            partial.at[a, order[2 * k], part],
+            pair_in.at[a, k, part],
+            pair_send.at[stage, k],
+            pair_recv.at[stage, k],
             {"tp": partner},
         )
 
-    def cross_copy(a):
+    def cross_copy(stage):
+        a, part = stages[stage]
         return remote(
-            cross_out.at[a], cross_in.at[a], cross_send.at[a], cross_recv.at[a], {"tp": across}
+            cross_out.at[a, part],
+            cross_in.at[a, part],
+            cross_send.at[stage],
+            cross_recv.at[stage],
+            {"tp": across},
+        )
+
+    def cross_over(stage):
+        a, part = stages[stage]
+        pair_copy(stage, 0).wait_recv()
+        cross_out[a, part] = (
+            partial[a, order[1], part].astype(WIDE) + pair_in[a, 0, part].astype(WIDE)
+        ).astype(LOW)
+        cross_copy(stage).start()
+
+    def summed(stage):
+        a, part = stages[stage]
+        pair_copy(stage, 1).wait_recv()
+        cross_copy(stage).wait_recv()
+        return (
+            partial[a, t, part].astype(WIDE)
+            + pair_in[a, 1, part].astype(WIDE)
+            + cross_in[a, part].astype(WIDE)
         )
 
     returns_arrived(0)
@@ -635,123 +762,122 @@
             partial[0, quarter, :, tile_of(j, tile)] = dot(back[0], w_out[:, at]).astype(LOW)
             return carry
 
-        lax.fori_loop(0, tiles, value_step, 0)
+        lax.fori_loop(0, tiles, value_step, 0, unroll=True)
         if k % 2 == 0:
             pair_copy(0, k // 2).start()
-    pair_copy(0, 0).wait_recv()
-    cross_out[0] = (partial[0, order[1]].astype(WIDE) + pair_in[0, 0].astype(WIDE)).astype(LOW)
-    cross_copy(0).start()
-
-    for a, weight in ((1, w_query), (2, w_value)):
+    cross_over(0)
+    sent_back(1)
+    for i in reversed(range(blocks)):
+        send_back(3, i)
+
+    weights = {1: w_query, 2: w_value, 3: w_key}
+
+    def dots_copy(half, offset):
+        return remote(
+            dots_out.at[half],
+            dots_in.at[half, offset],
+            dots_send.at[half, offset],
+            dots_recv.at[half, offset],
+            {"tp": lax.rem(t + offset, tp_size)},
+        )
+
+    def share_gradient(half, product):
+        stage = 1 + half
+        part = stages[stage][1]
+        dots = jnp.zeros((half_rows, 1), WIDE)
+        for k in range(tp_size):
+            quarter = order[k]
+            for j in range(tiles):
+                at = tile_of(quarter * tiles + j, tile)
+                here = tile_of(j, tile)
+                whole = product(quarter, at, here)
+                partial[1, quarter, part, here] = whole.astype(LOW)
+                inner = gain[:, at] * whole * wide[quarter, part, here].astype(WIDE)
+                dots += jnp.sum(inner, 1, keepdims=True)
+            if k % 2 == 0:
+                pair_copy(stage, k // 2).start()
+            if k == 2:
+                cross_over(stage)
+        dots_out[half] = jnp.broadcast_to(to_row(dots, rows), dots_out.shape[1:])
+        for offset in range(1, tp_size):
+            dots_copy(half, offset).start()
+        return dots
+
+    def finish_gradient(half, dots):
+        stage = 1 + half
+        part = stages[stage][1]
+        for offset in range(1, tp_size):
+            dots_copy(half, offset).wait_recv()
+            dots += to_column(dots_in[half, offset, :1], half_rows)
+        rinv = rinv_column[part, :]
+        out_grad[part, :] = (
+            wide_grad[t, part].astype(WIDE)
+            + rinv * gain[:, tile_of(t, columns)] * summed(stage)
+            - wide[t, part].astype(WIDE) * (rinv**3 * dots / model_width)
+        )
+
+    for a in (1, 2):
         returns_arrived(a)
-        for quarter in range(tp_size):
-
-            def grad_in_step(j, carry):
+
+        def quarter_step(quarter, carry):
+            for j in range(tiles):
                 at = tile_of(quarter * tiles + j, tile)
-                more = dot_last(back[a], weight[at, :])
                 here = tile_of(j, tile)
+                more = dot_last(back[a], weights[a][at, :])
                 if a == 1:
                     grad_sum[quarter, :, here] = more
                 else:
                     grad_sum[quarter, :, here] += more
-                return carry
-
-            lax.fori_loop(0, tiles, grad_in_step, 0)
+            return carry
+
+        lax.fori_loop(0, tp_size, quarter_step, 0)
+        if a == 1:
+            sent_back(2)
+            for i in reversed(range(blocks)):
+                send_back(4, i)
+    out_value[...] = jnp.where(
+        row_valid > 0.5, wide[t].astype(WIDE) + summed(0), 0.0
+    ).astype(LOW)
+
+    def product_of(half):
+        part = stages[1 + half][1]
+
+        def product(quarter, at, here):
+            return grad_sum[quarter, part, here] + dot_last(back[3, part], w_key[at, :])
+
+        return product
+
     returns_arrived(3)
-    dots = jnp.zeros((rows, 1), WIDE)
-    for k in range(tp_size):
-        quarter = order[k]
-
-        def last_step(j, dots):
-            at = tile_of(quarter * tiles + j, tile)
-            here = tile_of(j, tile)
-            whole = grad_sum[quarter, :, here] + dot_last(back[3], w_key[at, :])
-            partial[1, quarter, :, here] = whole.astype(LOW)
-            inner = gain[:, at] * whole * wide[quarter, :, here].astype(WIDE)
-            return dots + jnp.sum(inner, 1, keepdims=True)
-
-        dots = lax.fori_loop(0, tiles, last_step, dots)
-        if k % 2 == 0:
-            pair_copy(1, k // 2).start()
-        if k == 1:
-            pair_copy(1, 0).wait_recv()
-            cross_out[1] = (
-                partial[1, order[1]].astype(WIDE) + pair_in[1, 0].astype(WIDE)
-            ).astype(LOW)
-            cross_copy(1).start()
-
-    def dots_copy(offset):
-        return remote(
-            dots_out,
-            dots_in.at[offset],
-            dots_send.at[offset],
-            dots_recv.at[offset],
-            {"tp": lax.rem(t + offset, tp_size)},
-        )
-
-    dots_out[...] = jnp.broadcast_to(to_row(dots), dots_out.shape)
-    for offset in range(1, tp_size):
-        dots_copy(offset).start()
-
-    wide_in = wide[t].astype(WIDE)
-    rinv = rinv_column[...]
-    pair_copy(0, 1).wait_recv()
-    cross_copy(0).wait_recv()
-    total_value = (
-        partial[0, t].astype(WIDE) + pair_in[0, 1].astype(WIDE) + cross_in[0].astype(WIDE)
-    )
-    out_value[...] = jnp.where(row_valid > 0.5, wide_in + total_value, 0.0).astype(LOW)
-    for offset in range(1, tp_size):
-        dots_copy(offset).wait_recv()
-        dots += to_column(dots_in[offset][:1])
-    pair_copy(1, 1).wait_recv()
-    cross_copy(1).wait_recv()
-    total_grad = (
-        partial[1, t].astype(WIDE) + pair_in[1, 1].astype(WIDE) + cross_in[1].astype(WIDE)
-    )
-    out_grad[...] = (
-        wide_grad[t].astype(WIDE)
-        + rinv * gain[:, tile_of(t, columns)] * total_grad
-        - wide_in * (rinv**3 * dots / model_width)
-    )
+    upper_dots = share_gradient(0, product_of(0))
+    returns_arrived(4)
+    lower_dots = share_gradient(1, product_of(1))
+    finish_gradient(0, upper_dots)
+    finish_gradient(1, lower_dots)
 
     @pl.when(has_before)
     def _():
         lead_copy.wait_send()
 
     gather_drain(0, group_view)
-    for p in range(2):
+    for p in range(grad_pieces):
         gather_drain(1 + p, grad_views[p])
 
-    def drain_step(j, carry):
-        gather_drain(3 + j, wide_view(j))
-        return carry
-
-    lax.fori_loop(0, tiles, drain_step, 0)
+    for batch in range(2):
+        for j in range(2):
+            gather_drain(wide_chunk(batch, j), wide_view(batch, j))
     for offset in range(1, seq_size):
         peer = lax.rem(mine + offset, seq_size)
-        for a in range(heads.shape[0]):
-            remote(
-                outbox.at[a, peer],
-                heads.at[a, own_rows],
-                out_send.at[a, peer],
-                out_recv.at[a, mine],
-                {"seq": peer},
-            ).wait_send()
-        for a in range(returned):
-            remote(
-                returns.at[a, tile_of(peer, rows)],
-                back.at[a, :, own_columns],
-                back_send.at[a, peer],
-                back_recv.at[a, mine],
-                {"seq": peer},
-            ).wait_send()
-    for a in range(2):
+        for k in range(7):
+            head_copy(k, peer).wait_send()
+    for k in (3, 4):
+        sent_back(k)
+    for stage in range(len(stages)):
         for k in range(2):
-            pair_copy(a, k).wait_send()
-        cross_copy(a).wait_send()
-    for offset in range(1, tp_size):
-        dots_copy(offset).wait_send()
+            pair_copy(stage, k).wait_send()
+        cross_copy(stage).wait_send()
+    for half in range(2):
+        for offset in range(1, tp_size):
+            dots_copy(half, offset).wait_send()
 
 
 def per_device_whole(encoded, starts, w_up, norm_gain, w_query, w_key, w_value, w_out, cotangent):
@@ -762,9 +888,14 @@
     cap = starts.shape[1]
     total = starts.size
     tile = 2 * HEAD_DIM
-    chunks = 3 + columns // tile
+    chunks = 9
+    blocks = total // tile
     dma = pltpu.SemaphoreType.DMA
     scratch = [
+        pltpu.VMEM(starts.shape, jnp.int32),
+        pltpu.VMEM((1, model_width), WIDE),
+        pltpu.VMEM(encoded.shape, LOW),
+        pltpu.VMEM(cotangent.shape, LOW),
         pltpu.VMEM(w_up.shape, LOW),
         pltpu.VMEM(w_query.shape, LOW),
         pltpu.VMEM(w_key.shape, LOW),
@@ -777,13 +908,15 @@
         pltpu.VMEM((tp_size, rows, columns), LOW),
         pltpu.VMEM((tp_size, rows, columns), LOW),
         pltpu.VMEM((total, 1), WIDE),
+        pltpu.VMEM((total, 128), WIDE),
         pltpu.VMEM((rows, 1), WIDE),
         pltpu.VMEM((4, seq_size, rows, HEAD_DIM), LOW),
         pltpu.VMEM((4, total, HEAD_DIM), LOW),
         pltpu.VMEM((HEAD_DIM, total), LOW),
         pltpu.VMEM((HEAD_DIM, total), LOW),
-        pltpu.VMEM((total, tile), WIDE),
-        pltpu.VMEM((total, tile), WIDE),
+        pltpu.VMEM((blocks * (blocks + 1) // 2 * tile, tile), WIDE),
+        pltpu.VMEM((HEAD_DIM, total), WIDE),
+        pltpu.VMEM((1, total), WIDE),
         pltpu.VMEM((total, HEAD_DIM), WIDE),
         pltpu.VMEM((total, HEAD_DIM), WIDE),
         pltpu.VMEM((4, total, HEAD_DIM), LOW),
@@ -793,22 +926,23 @@
         pltpu.VMEM((2, 2, rows, columns), LOW),
         pltpu.VMEM((2, rows, columns), LOW),
         pltpu.VMEM((2, rows, columns), LOW),
-        pltpu.VMEM((8, rows), WIDE),
-        pltpu.VMEM((tp_size, 8, rows), WIDE),
+        pltpu.VMEM((2, 8, rows), WIDE),
+        pltpu.VMEM((2, tp_size, 8, rows), WIDE),
         dma((5, 4)),
+        dma((4,)),
         dma((2,)),
         dma((3, chunks)),
         dma((3, chunks)),
-        dma((4, seq_size)),
-        dma((4, seq_size)),
-        dma((4, seq_size)),
-        dma((4, seq_size)),
-            dma((2, 2)),
-        dma((2, 2)),
-        dma((2,)),
-        dma((2,)),
-        dma((tp_size,)),
-        dma((tp_size,)),
+        dma((7, seq_size)),
+        dma((7, seq_size)),
+        dma((5, seq_size)),
+        dma((5, seq_size)),
+        dma((3, 2)),
+        dma((3, 2)),
+        dma((3,)),
+        dma((3,)),
+        dma((2, tp_size)),
+        dma((2, tp_size)),
     ]
     near = pl.BlockSpec(memory_space=pltpu.VMEM)
     far = pl.BlockSpec(memory_space=pl.ANY)
@@ -819,16 +953,16 @@
                 jax.ShapeDtypeStruct((rows, columns), LOW),
                 jax.ShapeDtypeStruct((rows, columns), WIDE),
             ],
-            in_specs=[near] * 4 + [far] * 5,
+            in_specs=[far] * 9,
             out_specs=[near] * 2,
             scratch_shapes=scratch,
             compiler_params=pltpu.CompilerParams(
                 collective_id=0, has_side_effects=True, vmem_limit_bytes=67043328
             ),
         )(
-            encoded,
             starts,
             norm_gain.reshape(1, model_width),
+            encoded,
             cotangent,
             w_up,
             w_query,

time: 104 us -> 81.5 us (0.78)
  Pallas kernels: 99.4 us -> 77.1 us
    pallas_call x1, Pallas kernels: 99.4 us -> 77.1 us  [per_device_whole(): pl.pallas_call(functools.partial(layer_kernel, seq_size, tp_size), out_sh...]
where the time goes in v2:
time: 81.5 us; the launch traced here: 81.3 us
  Pallas kernels  77.1 us (95%)
  local copies, waits for them, and re-layouts  3.55 us (4%)
    pallas_call x1, Pallas kernels, per_device_whole(): pl.pallas_call(functools.partial(layer_kernel, seq_size, tp_size), out_sh...  77.1 us
    unnamed x2, local copies, waits for them, and re-layouts  3.55 us

profile of v2, /device:TPU:0, one launch (start us, length us, event | category | flops | bytes accessed | tf_op | source)
XLA Modules:
  0.0 81.3 jit_solution(10657087375206389042)
XLA Ops:
  0.6 77.1 %shard_map.104 = (bf16[128,1024]{1,0:T(8,128)(2,1)}, f32[128,1024]{1,0:T(8,128)}) custom-call(s32[32,32]{1,0:T(8,128)} %starts_far.1, f32[1,4096]{1,0:T(1,128)} %bitcast.1, bf16[256,1280]{1,0:T(8,128)(2,1)} %encoded_far.1, bf16[128,1024]{1,0:T(8,128)(2,1)} %cotangent_far.1, bf16[1280,1024]{1,0:T(8,128)(2,1)} %w_up_far.1, bf16[4096,1024]{1,0:T(8,128)(2,1)} %w_query_far.1, ...), custom_call_target="tpu_custom_call" | custom-call | tf_op jit(solution)/shard_map/pallas_call | solution.py:950
  77.7 1.7 %copy.13 = bf16[128,1024]{1,0:T(8,128)(2,1)} copy(bf16[128,1024]{1,0:T(8,128)(2,1)} %get-tuple-element.4) | data formatting | bytes 524288
  79.4 1.9 %copy.14 = f32[128,1024]{1,0:T(8,128)} copy(f32[128,1024]{1,0:T(8,128)} %get-tuple-element.5) | data formatting | bytes 1048576

commit v3 on v2

--- a/solution.py
+++ b/solution.py
@@ -312,22 +312,17 @@
     ]
     for copy in near_copies:
         copy.start()
-    pieces = weight_sem.shape[1]
+    pieces = 4
 
     def weight_copies(i, far, near):
         depth = far.shape[0] // pieces
-        return [
-            pltpu.make_async_copy(
-                far.at[pl.ds(p * depth, depth)], near.at[pl.ds(p * depth, depth)], weight_sem.at[i, p]
-            )
-            for p in range(pieces)
-        ]
-
-    up_copies = weight_copies(0, w_up_far, w_up)
-    out_copies = weight_copies(1, w_out_far, w_out)
-    key_copies = weight_copies(2, w_key_far, w_key)
-    query_copies = weight_copies(3, w_query_far, w_query)
-    value_copies = weight_copies(4, w_value_far, w_value)
+        for p in range(pieces):
+            part = pl.ds(p * depth, depth)
+            pltpu.make_async_copy(far.at[part], near.at[part], weight_sem.at[i]).start()
+
+    def weight_wait(i, far, near):
+        pltpu.make_async_copy(far, near, weight_sem.at[i]).wait()
+
     near_copies[0].wait()
     limit = float(byte_rows)
     own = starts[pl.ds(shard, 1), :].astype(WIDE)
@@ -340,10 +335,70 @@
     lead_places = lax.broadcasted_iota(jnp.int32, (16, byte_rows), 1).astype(WIDE)
     leading = jnp.where(lead_places < own[:, :1], 1.0, 0.0).astype(LOW)
     near_copies[1].wait()
-    for copy in up_copies:
-        copy.start()
+    weight_copies(0, w_up_far, w_up)
     lead_out[...] = dot(leading, encoded[...])[:1]
     sums = dot(inside, encoded[...])
+
+    neighbours = group_first.astype(jnp.int32) + group_last.astype(jnp.int32)
+    pl.semaphore_wait(barrier, tp_size + seq_size - 2 + neighbours)
+
+    lead_copy = remote(lead_out, lead_in, lead_sem.at[0], lead_sem.at[1], shard_before)
+
+    @pl.when(has_before)
+    def _():
+        lead_copy.start()
+
+    def gather_copy(way, k, kind, piece):
+        target = across if way == 0 else partner
+        return remote(
+            piece, piece, gather_send.at[kind], gather_recv.at[way, k], {"tp": target}
+        )
+
+    def gather_start(k, kind, view):
+        gather_copy(0, k, kind, view(t)).start()
+        gather_copy(1, k, kind, view(t)).start()
+
+    def gather_relay(k, kind, view):
+        gather_copy(0, k, kind, view(across)).wait_recv()
+        gather_copy(2, k, kind, view(across)).start()
+
+    def gather_finish(k, kind, view, ways=(1, 2)):
+        for way in ways:
+            gather_copy(way, k, kind, view(partner if way == 1 else diagonal)).wait_recv()
+
+    grad_view = lambda q: wide_grad.at[q]
+    group_view = lambda q: group.at[tile_of(q, cap)]
+    half_rows = rows // 2
+    wide_tile = columns // 2
+
+    def wide_view(batch, j):
+        def view(q):
+            of_chip = q // 2
+            place = of_chip if batch == 0 else 1 - of_chip
+            return wide.at[
+                q, tile_of(place, half_rows), j * wide_tile : (j + 1) * wide_tile
+            ]
+
+        return view
+
+    def wide_chunk(batch, j):
+        return 2 + 2 * batch + j
+
+    @pl.when(has_after)
+    def _():
+        lead_copy.wait_recv()
+
+    joined = jnp.where(
+        jnp.logical_and(first < limit, following >= limit), jnp.where(has_after, 1.0, 0.0), 0.0
+    )
+    sums = sums + joined * jnp.where(has_after, lead_in[...], 0.0)
+    sizes = (following - first) * jnp.where(first < limit, 1.0, 0.0) + joined * after[:, :1]
+    group[tile_of(t, cap), :] = (sums / jnp.maximum(sizes, 1.0)).astype(LOW)
+    gather_start(0, 0, group_view)
+    weight_copies(1, w_key_far, w_key)
+    weight_copies(2, w_query_far, w_query)
+    weight_copies(3, w_value_far, w_value)
+    weight_copies(4, w_out_far, w_out)
 
     index = lax.broadcasted_iota(jnp.int32, (patches_total, shards), 0)
     lane = lax.broadcasted_iota(jnp.int32, (patches_total, shards), 1)
@@ -360,100 +415,19 @@
     key_bias[...] = jnp.broadcast_to((valid_column[...] - 1.0) * -NEG, key_bias.shape)
     near_copies[2].wait()
     wide_grad[t] = jnp.where(row_valid > 0.5, cotangent[...].astype(WIDE), 0.0).astype(LOW)
-    near_copies[3].wait()
-
-    neighbours = group_first.astype(jnp.int32) + group_last.astype(jnp.int32)
-    pl.semaphore_wait(barrier, tp_size + seq_size - 2 + neighbours)
-
-    lead_copy = remote(lead_out, lead_in, lead_sem.at[0], lead_sem.at[1], shard_before)
-
-    @pl.when(has_before)
-    def _():
-        lead_copy.start()
-
-    def gather_start(k, view):
-        piece = view(t)
-        remote(
-            piece, piece, gather_send.at[0, k], gather_recv.at[0, k], {"tp": across}
-        ).start()
-        remote(
-            piece, piece, gather_send.at[1, k], gather_recv.at[1, k], {"tp": partner}
-        ).start()
-
-    def gather_relay(k, view):
-        piece = view(across)
-        remote(
-            piece, piece, gather_send.at[0, k], gather_recv.at[0, k], {"tp": across}
-        ).wait_recv()
-        remote(
-            piece, piece, gather_send.at[2, k], gather_recv.at[2, k], {"tp": partner}
-        ).start()
-
-    def gather_finish(k, view, ways=(1, 2)):
-        for way in ways:
-            piece = view(partner if way == 1 else diagonal)
-            remote(
-                piece, piece, gather_send.at[way, k], gather_recv.at[way, k], {"tp": partner}
-            ).wait_recv()
-
-    def gather_drain(k, view):
-        for way, origin, target in ((0, t, across), (1, t, partner), (2, across, partner)):
-            piece = view(origin)
-            remote(
-                piece, piece, gather_send.at[way, k], gather_recv.at[way, k], {"tp": target}
-            ).wait_send()
-
-    grad_pieces = 4
-    piece_rows = rows // grad_pieces
-    grad_views = [
-        lambda q, p=p: wide_grad.at[q, pl.ds(p * piece_rows, piece_rows)]
-        for p in range(grad_pieces)
-    ]
-    group_view = lambda q: group.at[tile_of(q, cap)]
-    half_rows = rows // 2
-    wide_tile = columns // 2
-
-    def wide_view(batch, j):
-        def view(q):
-            of_chip = q // 2
-            place = of_chip if batch == 0 else 1 - of_chip
-            return wide.at[
-                q, tile_of(place, half_rows), j * wide_tile : (j + 1) * wide_tile
-            ]
-
-        return view
-
-    def wide_chunk(batch, j):
-        return 1 + grad_pieces + 2 * batch + j
-
-    @pl.when(has_after)
-    def _():
-        lead_copy.wait_recv()
-
-    joined = jnp.where(
-        jnp.logical_and(first < limit, following >= limit), jnp.where(has_after, 1.0, 0.0), 0.0
-    )
-    sums = sums + joined * jnp.where(has_after, lead_in[...], 0.0)
-    sizes = (following - first) * jnp.where(first < limit, 1.0, 0.0) + joined * after[:, :1]
-    group[tile_of(t, cap), :] = (sums / jnp.maximum(sizes, 1.0)).astype(LOW)
-    gather_start(0, group_view)
-    for copies in (key_copies, query_copies, value_copies, out_copies):
-        for copy in copies:
-            copy.start()
 
     def raise_rows(batch):
         place = tile_of(chip if batch == 0 else 1 - chip, half_rows)
         for j in range(2):
             cut = slice(j * wide_tile, (j + 1) * wide_tile)
             wide[t, place, cut] = dot(group[place, :], w_up[:, cut]).astype(LOW)
-            gather_start(wide_chunk(batch, j), wide_view(batch, j))
-
-    gather_finish(0, group_view, (1,))
-    for copy in up_copies:
-        copy.wait()
+            gather_start(wide_chunk(batch, j), 2, wide_view(batch, j))
+
+    gather_finish(0, 0, group_view, (1,))
+    weight_wait(0, w_up_far, w_up)
     raise_rows(0)
-    gather_relay(0, group_view)
-    gather_finish(0, group_view, (2,))
+    gather_relay(0, 0, group_view)
+    gather_finish(0, 0, group_view, (2,))
     raise_rows(1)
 
     far_half = 1 - mine // (seq_size // 2)
@@ -469,8 +443,8 @@
         return remote(
             src,
             heads.at[3 if k == 6 else k // 2, place],
-            out_send.at[k, h],
-            out_recv.at[k, mine],
+            out_send.at[k],
+            out_recv.at[k],
             {"seq": h},
         )
 
@@ -479,9 +453,9 @@
         def _():
             head_copy(k, h).start()
 
-    def keep_heads(a, j, block, start, size):
-        for u in range(2):
-            h = 2 * j + u
+    def keep_heads(a, h_first, block, start, size):
+        for u in range(block.shape[1] // HEAD_DIM):
+            h = h_first + u
             part = block[:, u * HEAD_DIM : (u + 1) * HEAD_DIM]
 
             @pl.when(h == mine)
@@ -497,7 +471,7 @@
 
     def relay_rows(batch):
         for j in range(2):
-            gather_relay(wide_chunk(batch, j), wide_view(batch, j))
+            gather_relay(wide_chunk(batch, j), 2, wide_view(batch, j))
 
     def norm_rows(batch):
         place = tile_of(1 - chip if batch == 0 else chip, half_rows)
@@ -510,55 +484,51 @@
         square = lax.fori_loop(0, tp_size, norm_step, jnp.zeros((half_rows, 1), WIDE))
         rinv_column[place, :] = lax.rsqrt(square / model_width + EPS)
 
-    def project(a, weight, batch):
+    def project(a, weight, batch, width):
         piece = 1 - chip if batch == 0 else chip
         place = tile_of(piece, half_rows)
+        steps = columns // width
+        held = width // HEAD_DIM
 
         def step(jj, carry):
-            j = tile_order(jj)
-            acc = jnp.zeros((half_rows, tile), WIDE)
+            j = lax.rem(far_half * (steps // 2) + jj, steps)
+            acc = jnp.zeros((half_rows, width), WIDE)
             for q in range(tp_size):
                 acc += dot(
-                    scaled[q, place], weight[q * columns : (q + 1) * columns, tile_of(j, tile)]
+                    scaled[q, place], weight[q * columns : (q + 1) * columns, tile_of(j, width)]
                 )
             block = (rinv_column[place, :] * acc).astype(LOW)
-            keep_heads(a, j, block, piece * half_rows, half_rows)
-            for u in range(2):
-                start_head(2 * a + batch, 2 * j + u)
+            keep_heads(a, j * held, block, piece * half_rows, half_rows)
+            for u in range(held):
+                start_head(2 * a + batch, j * held + u)
             return carry
 
-        lax.fori_loop(0, tiles, step, 0)
-
+        lax.fori_loop(0, steps, step, 0)
+
+    near_copies[3].wait()
     relay_rows(0)
     for j in range(2):
-        gather_finish(wide_chunk(0, j), wide_view(0, j), (2,))
-        gather_finish(wide_chunk(1, j), wide_view(1, j), (1,))
+        gather_finish(wide_chunk(0, j), 2, wide_view(0, j), (2,))
+        gather_finish(wide_chunk(1, j), 2, wide_view(1, j), (1,))
     norm_rows(0)
-    for copy in key_copies:
-        copy.wait()
-    project(1, w_key, 0)
+    weight_wait(1, w_key_far, w_key)
+    project(1, w_key, 0, tile)
     relay_rows(1)
-    for p in range(grad_pieces):
-        gather_start(1 + p, grad_views[p])
-    for copy in query_copies:
-        copy.wait()
-    project(0, w_query, 0)
-    for copy in value_copies:
-        copy.wait()
-    project(2, w_value, 0)
+    gather_start(1, 1, grad_view)
+    weight_wait(2, w_query_far, w_query)
+    project(0, w_query, 0, wide_tile)
+    weight_wait(3, w_value_far, w_value)
+    project(2, w_value, 0, wide_tile)
     for j in range(2):
-        gather_finish(wide_chunk(0, j), wide_view(0, j), (1,))
-        gather_finish(wide_chunk(1, j), wide_view(1, j), (2,))
+        gather_finish(wide_chunk(0, j), 2, wide_view(0, j), (1,))
+        gather_finish(wide_chunk(1, j), 2, wide_view(1, j), (2,))
     norm_rows(1)
-    project(1, w_key, 1)
-    project(0, w_query, 1)
-    for p in range(grad_pieces):
-        gather_relay(1 + p, grad_views[p])
-    project(2, w_value, 1)
-    for copy in out_copies:
-        copy.wait()
-    for p in range(grad_pieces):
-        gather_finish(1 + p, grad_views[p])
+    project(1, w_key, 1, wide_tile)
+    project(0, w_query, 1, wide_tile)
+    gather_relay(1, 1, grad_view)
+    project(2, w_value, 1, wide_tile)
+    weight_wait(4, w_out_far, w_out)
+    gather_finish(1, 1, grad_view)
 
     def d_attn_step(jj, carry):
         j = tile_order(jj)
@@ -567,29 +537,34 @@
             acc += dot_last(
                 wide_grad[q], w_out[tile_of(j, tile), q * columns : (q + 1) * columns]
             )
-        keep_heads(3, j, acc.astype(LOW), 0, rows)
+        keep_heads(3, 2 * j, acc.astype(LOW), 0, rows)
+        for u in range(2):
+            start_head(6, 2 * j + u)
         return carry
 
     lax.fori_loop(0, tiles, d_attn_step, 0)
 
 
     def heads_arrived(k):
-        for offset in range(1, seq_size):
-            source = lax.rem(mine + offset, seq_size)
-            if k == 6:
-                place = heads.at[3, tile_of(source, rows)]
-            else:
-                piece = 1 - chip if k % 2 == 0 else chip
-                place = heads.at[k // 2, tile_of(2 * source + piece, half_rows)]
-            remote(
-                place, place, out_send.at[k, source], out_recv.at[k, source], {"seq": source}
-            ).wait_recv()
-
-    for k in (2, 0, 4, 3, 1):
+        size = (rows if k == 6 else half_rows) * (seq_size - 1)
+        place = heads.at[3 if k == 6 else k // 2, :size]
+        remote(place, place, out_send.at[k], out_recv.at[k], {"seq": mine}).wait_recv()
+
+    def turn_square(q, carry):
+        steps = columns // tile
+        for i in range(steps):
+            for j in range(i, steps):
+                upper = w_key.at[tile_of(q * steps + i, tile), j * tile : (j + 1) * tile]
+                lower = w_key.at[tile_of(q * steps + j, tile), i * tile : (i + 1) * tile]
+                turned = upper[...].T
+                if i != j:
+                    upper[...] = lower[...].T
+                lower[...] = turned
+        return carry
+
+    lax.fori_loop(0, tp_size, turn_square, 0)
+    for k in range(4):
         heads_arrived(k)
-    for step in range(seq_size):
-        start_head(6, lax.rem(far_half * (seq_size // 2) + step, seq_size))
-    heads_arrived(5)
 
     blocks = patches_total // tile
     own_columns = tile_of(mine, HEAD_DIM)
@@ -598,14 +573,17 @@
         if k < 3:
             return k, 0, rows
         return 3, half_rows * (k - 3), half_rows
+
+    half_seq = seq_size // 2
+    near_half = mine // half_seq
 
     def return_copy(k, peer):
         a, start, size = piece_of(k)
         return remote(
             returns.at[a, pl.ds(peer * rows + start, size)],
             back.at[a, start : start + size, own_columns],
-            back_send.at[k, peer],
-            back_recv.at[k, mine],
+            back_send.at[k],
+            back_recv.at[k, jnp.where(peer // half_seq == near_half, 0, 1)],
             {"seq": peer},
         )
 
@@ -623,11 +601,9 @@
                 back[a, start : start + size, own_columns] = returns[a, first : first + size, :]
 
     def sent_back(k):
-        for peer in range(seq_size):
-
-            @pl.when(peer != mine)
-            def _():
-                return_copy(k, peer).wait_send()
+        a, start, size = piece_of(k)
+        sent = returns.at[a, : size * (seq_size - 1)]
+        remote(sent, sent, back_send.at[k], back_recv.at[k, 0], {"seq": mine}).wait_send()
 
     def cut_of(i):
         return slice(i * tile, (i + 1) * tile)
@@ -637,7 +613,6 @@
 
     for j in range(blocks):
         key_turned[:, cut_of(j)] = heads[1, cut_of(j), :].astype(WIDE).T.astype(LOW)
-        value_turned[:, cut_of(j)] = heads[2, cut_of(j), :].astype(WIDE).T.astype(LOW)
 
     def attend(i):
         peak = jnp.full((1, tile), NEG, WIDE)
@@ -652,14 +627,17 @@
             scores[score_cut(i, j), :] = score
             peak = jnp.maximum(peak, jnp.max(score, 0, keepdims=True))
         total = jnp.zeros((1, tile), WIDE)
-        mixed = jnp.zeros((HEAD_DIM, tile), WIDE)
         for j in range(i + 1):
             expo = jnp.exp(scores[score_cut(i, j), :] - peak)
             scores[score_cut(i, j), :] = expo
             total += jnp.sum(expo, 0, keepdims=True)
-            mixed += dot(value_turned[:, cut_of(j)], expo.astype(LOW))
         share_row[:, cut_of(i)] = 1.0 / total
-        attn = (mixed / total).astype(LOW).astype(WIDE)
+
+    def mix(i):
+        mixed = jnp.zeros((HEAD_DIM, tile), WIDE)
+        for j in range(i + 1):
+            mixed += dot(value_turned[:, cut_of(j)], scores[score_cut(i, j), :].astype(LOW))
+        attn = (mixed * share_row[:, cut_of(i)]).astype(LOW).astype(WIDE)
         attn_turned[:, cut_of(i)] = attn
         returns[0, cut_of(i), :] = attn.T.astype(LOW)
 
@@ -687,8 +665,14 @@
         returns[1, cut_of(i), :] = (query_sum * scale).T.astype(LOW)
 
     ends = [0] + list(reversed(range(1, blocks)))
+    for i in range(blocks):
+        attend(i)
+    for k in (4, 5):
+        heads_arrived(k)
+    for j in range(blocks):
+        value_turned[:, cut_of(j)] = heads[2, cut_of(j), :].astype(WIDE).T.astype(LOW)
     for i in ends:
-        attend(i)
+        mix(i)
         send_back(0, i)
     heads_arrived(6)
     for i in reversed(range(blocks)):
@@ -698,13 +682,12 @@
     for i in reversed(range(blocks)):
         send_back(2, i)
 
-    def returns_arrived(k):
+    def returns_arrived(k, sides=(0, 1)):
         a, start, size = piece_of(k)
-        for step in range(1, seq_size):
-            source = lax.rem(mine + step, seq_size)
-            place = back.at[a, start : start + size, tile_of(source, HEAD_DIM)]
+        for side in sides:
+            place = returns.at[a, : size * (half_seq - 1 + side)]
             remote(
-                place, place, back_send.at[k, source], back_recv.at[k, source], {"seq": source}
+                place, place, back_send.at[k], back_recv.at[k, side], {"seq": mine}
             ).wait_recv()
 
     order = (
@@ -720,7 +703,7 @@
         return remote(
             partial.at[a, order[2 * k], part],
             pair_in.at[a, k, part],
-            pair_send.at[stage, k],
+            pair_send.at[stage],
             pair_recv.at[stage, k],
             {"tp": partner},
         )
@@ -757,27 +740,20 @@
     for k in range(tp_size):
         quarter = order[k]
 
-        def value_step(j, carry):
-            at = tile_of(quarter * tiles + j, tile)
-            partial[0, quarter, :, tile_of(j, tile)] = dot(back[0], w_out[:, at]).astype(LOW)
-            return carry
-
-        lax.fori_loop(0, tiles, value_step, 0, unroll=True)
+        for j in range(2):
+            at = tile_of(quarter * 2 + j, wide_tile)
+            here = slice(j * wide_tile, (j + 1) * wide_tile)
+            partial[0, quarter, :, here] = dot(back[0], w_out[:, at]).astype(LOW)
         if k % 2 == 0:
             pair_copy(0, k // 2).start()
-    cross_over(0)
-    sent_back(1)
-    for i in reversed(range(blocks)):
-        send_back(3, i)
-
     weights = {1: w_query, 2: w_value, 3: w_key}
 
     def dots_copy(half, offset):
         return remote(
             dots_out.at[half],
             dots_in.at[half, offset],
-            dots_send.at[half, offset],
-            dots_recv.at[half, offset],
+            dots_send.at[half],
+            dots_recv.at[half],
             {"tp": lax.rem(t + offset, tp_size)},
         )
 
@@ -787,10 +763,10 @@
         dots = jnp.zeros((half_rows, 1), WIDE)
         for k in range(tp_size):
             quarter = order[k]
-            for j in range(tiles):
-                at = tile_of(quarter * tiles + j, tile)
-                here = tile_of(j, tile)
-                whole = product(quarter, at, here)
+            for j in range(2):
+                at = tile_of(quarter * 2 + j, wide_tile)
+                here = slice(j * wide_tile, (j + 1) * wide_tile)
+                whole = product(quarter, here)
                 partial[1, quarter, part, here] = whole.astype(LOW)
                 inner = gain[:, at] * whole * wide[quarter, part, here].astype(WIDE)
                 dots += jnp.sum(inner, 1, keepdims=True)
@@ -806,8 +782,9 @@
     def finish_gradient(half, dots):
         stage = 1 + half
         part = stages[stage][1]
+        place = dots_in.at[half, 1:]
+        remote(place, place, dots_send.at[half], dots_recv.at[half], {"tp": t}).wait_recv()
         for offset in range(1, tp_size):
-            dots_copy(half, offset).wait_recv()
             dots += to_column(dots_in[half, offset, :1], half_rows)
         rinv = rinv_column[part, :]
         out_grad[part, :] = (
@@ -816,22 +793,29 @@
             - wide[t, part].astype(WIDE) * (rinv**3 * dots / model_width)
         )
 
-    for a in (1, 2):
-        returns_arrived(a)
+    half_columns = columns // 2
+    for a, side in ((1, 0), (1, 1), (2, 0), (2, 1)):
+        returns_arrived(a, (side,))
+        sources = tile_of(near_half if side == 0 else 1 - near_half, half_columns)
 
         def quarter_step(quarter, carry):
             for j in range(tiles):
                 at = tile_of(quarter * tiles + j, tile)
                 here = tile_of(j, tile)
-                more = dot_last(back[a], weights[a][at, :])
-                if a == 1:
+                more = dot_last(back[a, :, sources], weights[a][at, sources])
+                if a == 1 and side == 0:
                     grad_sum[quarter, :, here] = more
                 else:
                     grad_sum[quarter, :, here] += more
             return carry
 
-        lax.fori_loop(0, tp_size, quarter_step, 0)
-        if a == 1:
+        lax.fori_loop(0, tp_size, quarter_step, 0, unroll=2)
+        if a == 1 and side == 0:
+            sent_back(1)
+            for i in reversed(range(blocks)):
+                send_back(3, i)
+            cross_over(0)
+        if a == 1 and side == 1:
             sent_back(2)
             for i in reversed(range(blocks)):
                 send_back(4, i)
@@ -842,8 +826,9 @@
     def product_of(half):
         part = stages[1 + half][1]
 
-        def product(quarter, at, here):
-            return grad_sum[quarter, part, here] + dot_last(back[3, part], w_key[at, :])
+        def product(quarter, here):
+            turned = w_key[tile_of(quarter, columns), here]
+            return grad_sum[quarter, part, here] + dot(back[3, part], turned)
 
         return product
 
@@ -858,26 +843,23 @@
     def _():
         lead_copy.wait_send()
 
-    gather_drain(0, group_view)
-    for p in range(grad_pieces):
-        gather_drain(1 + p, grad_views[p])
-
-    for batch in range(2):
-        for j in range(2):
-            gather_drain(wide_chunk(batch, j), wide_view(batch, j))
-    for offset in range(1, seq_size):
-        peer = lax.rem(mine + offset, seq_size)
-        for k in range(7):
-            head_copy(k, peer).wait_send()
+    for kind, sent in ((0, group.at[: 3 * cap]), (1, wide_grad.at[:3]), (2, wide.at[:3])):
+        gather_copy(0, 0, kind, sent).wait_send()
+    for k in range(7):
+        sent = outbox.at[3, 1:] if k == 6 else outbox.at[k // 2, 1:, :half_rows]
+        remote(sent, sent, out_send.at[k], out_recv.at[k], {"seq": mine}).wait_send()
     for k in (3, 4):
         sent_back(k)
     for stage in range(len(stages)):
-        for k in range(2):
-            pair_copy(stage, k).wait_send()
+        a, part = stages[stage]
+        sent = pair_in.at[a, :, part]
+        remote(
+            sent, sent, pair_send.at[stage], pair_recv.at[stage, 0], {"tp": partner}
+        ).wait_send()
         cross_copy(stage).wait_send()
     for half in range(2):
-        for offset in range(1, tp_size):
-            dots_copy(half, offset).wait_send()
+        sent = dots_in.at[half, 1:]
+        remote(sent, sent, dots_send.at[half], dots_recv.at[half], {"tp": t}).wait_send()
 
 
 def per_device_whole(encoded, starts, w_up, norm_gain, w_query, w_key, w_value, w_out, cotangent):
@@ -888,7 +870,6 @@
     cap = starts.shape[1]
     total = starts.size
     tile = 2 * HEAD_DIM
-    chunks = 9
     blocks = total // tile
     dma = pltpu.SemaphoreType.DMA
     scratch = [
@@ -928,21 +909,21 @@
         pltpu.VMEM((2, rows, columns), LOW),
         pltpu.VMEM((2, 8, rows), WIDE),
         pltpu.VMEM((2, tp_size, 8, rows), WIDE),
-        dma((5, 4)),
+        dma((5,)),
         dma((4,)),
         dma((2,)),
-        dma((3, chunks)),
-        dma((3, chunks)),
-        dma((7, seq_size)),
-        dma((7, seq_size)),
-        dma((5, seq_size)),
-        dma((5, seq_size)),
-        dma((3, 2)),
+        dma((3,)),
+        dma((3, 6)),
+        dma((7,)),
+        dma((7,)),
+        dma((5,)),
+        dma((5, 2)),
+        dma((3,)),
         dma((3, 2)),
         dma((3,)),
         dma((3,)),
-        dma((2, tp_size)),
-        dma((2, tp_size)),
+        dma((2,)),
+        dma((2,)),
     ]
     near = pl.BlockSpec(memory_space=pltpu.VMEM)
     far = pl.BlockSpec(memory_space=pl.ANY)
@@ -950,14 +931,14 @@
         pl.pallas_call(
             functools.partial(layer_kernel, seq_size, tp_size),
             out_shape=[
-                jax.ShapeDtypeStruct((rows, columns), LOW),
-                jax.ShapeDtypeStruct((rows, columns), WIDE),
+                pltpu.VMEM((rows, columns), LOW),
+                pltpu.VMEM((rows, columns), WIDE),
             ],
             in_specs=[far] * 9,
             out_specs=[near] * 2,
             scratch_shapes=scratch,
             compiler_params=pltpu.CompilerParams(
-                collective_id=0, has_side_effects=True, vmem_limit_bytes=67043328
+                collective_id=0, has_side_effects=True, vmem_limit_bytes=60 * 1024 * 1024
             ),
         )(
             starts,

time: 81.5 us -> 74.6 us (0.915)
  Pallas kernels: 77.1 us -> 72.2 us
  local copies, waits for them, and re-layouts: 3.55 us -> 1.5 us
    pallas_call x1, Pallas kernels: 77.1 us -> 72.2 us  [per_device_whole(): pl.pallas_call(functools.partial(layer_kernel, seq_size, tp_size), out_sh...]
    unnamed x2, local copies, waits for them, and re-layouts: 3.55 us -> 1.5 us
where the time goes in v3:
time: 74.6 us; the launch traced here: 74.3 us
  Pallas kernels  72.2 us (97%)
  local copies, waits for them, and re-layouts  1.5 us (2%)
    pallas_call x1, Pallas kernels, per_device_whole(): pl.pallas_call(functools.partial(layer_kernel, seq_size, tp_size), out_sh...  72.2 us
    unnamed x2, local copies, waits for them, and re-layouts  1.5 us

profile of v3, /device:TPU:0, one launch (start us, length us, event | category | flops | bytes accessed | tf_op | source)
XLA Modules:
  0.0 74.3 jit_solution(10693610634337320162)
XLA Ops:
  0.6 72.2 %shard_map.104 = (bf16[128,1024]{1,0:T(8,128)(2,1)S(1)}, f32[128,1024]{1,0:T(8,128)S(1)}) custom-call(s32[32,32]{1,0:T(8,128)} %starts_far.1, f32[1,4096]{1,0:T(1,128)} %bitcast.1, bf16[256,1280]{1,0:T(8,128)(2,1)} %encoded_far.1, bf16[128,1024]{1,0:T(8,128)(2,1)} %cotangent_far.1, bf16[1280,1024]{1,0:T(8,128)(2,1)} %w_up_far.1, ...), custom_call_target="tpu_custom_call" | custom-call | tf_op jit(solution)/shard_map/pallas_call | solution.py:931
  72.8 0.7 copy.13
  73.5 0.8 %copy.14 = f32[128,1024]{1,0:T(8,128)} copy(f32[128,1024]{1,0:T(8,128)S(1)} %get-tuple-element.3) | data formatting | bytes 1048576

commit v4 on v3

--- a/solution.py
+++ b/solution.py
@@ -211,7 +211,6 @@
     wide,
     wide_grad,
     scaled,
-    valid_column,
     key_bias,
     rinv_column,
     outbox,
@@ -336,8 +335,18 @@
     leading = jnp.where(lead_places < own[:, :1], 1.0, 0.0).astype(LOW)
     near_copies[1].wait()
     weight_copies(0, w_up_far, w_up)
+    weight_copies(4, w_out_far, w_out)
     lead_out[...] = dot(leading, encoded[...])[:1]
     sums = dot(inside, encoded[...])
+
+    own_rows = tile_of(mine, rows)
+    own_starts = [
+        to_column(starts[pl.ds(mine * tp_size + u, 1), :].astype(WIDE), cap)
+        for u in range(tp_size)
+    ]
+    row_valid = jnp.where(jnp.concatenate(own_starts, 0) < limit, 1.0, 0.0)
+    near_copies[2].wait()
+    wide_grad[t] = jnp.where(row_valid > 0.5, cotangent[...].astype(WIDE), 0.0).astype(LOW)
 
     neighbours = group_first.astype(jnp.int32) + group_last.astype(jnp.int32)
     pl.semaphore_wait(barrier, tp_size + seq_size - 2 + neighbours)
@@ -366,9 +375,14 @@
         for way in ways:
             gather_copy(way, k, kind, view(partner if way == 1 else diagonal)).wait_recv()
 
-    grad_view = lambda q: wide_grad.at[q]
+    half_rows = rows // 2
+    grad_views = (
+        lambda q: wide_grad.at[q, :half_rows],
+        lambda q: wide_grad.at[q, half_rows:],
+    )
+    gather_start(1, 1, grad_views[0])
+
     group_view = lambda q: group.at[tile_of(q, cap)]
-    half_rows = rows // 2
     wide_tile = columns // 2
 
     def wide_view(batch, j):
@@ -398,23 +412,6 @@
     weight_copies(1, w_key_far, w_key)
     weight_copies(2, w_query_far, w_query)
     weight_copies(3, w_value_far, w_value)
-    weight_copies(4, w_out_far, w_out)
-
-    index = lax.broadcasted_iota(jnp.int32, (patches_total, shards), 0)
-    lane = lax.broadcasted_iota(jnp.int32, (patches_total, shards), 1)
-    owner = jnp.where((index >= lane * cap) & (index < lane * cap + cap), 1.0, 0.0).astype(LOW)
-    valid = jnp.where(starts[...].astype(WIDE) < limit, 1.0, 0.0).astype(LOW)
-    spread = dot(owner, valid)
-    slots = lax.broadcasted_iota(jnp.int32, (patches_total, cap), 1)
-    places_in = lax.broadcasted_iota(jnp.int32, (patches_total, cap), 0)
-    valid_column[...] = jnp.sum(
-        jnp.where(jnp.bitwise_and(places_in, cap - 1) == slots, spread, 0.0), 1, keepdims=True
-    )
-    own_rows = tile_of(mine, rows)
-    row_valid = valid_column[own_rows, :]
-    key_bias[...] = jnp.broadcast_to((valid_column[...] - 1.0) * -NEG, key_bias.shape)
-    near_copies[2].wait()
-    wide_grad[t] = jnp.where(row_valid > 0.5, cotangent[...].astype(WIDE), 0.0).astype(LOW)
 
     def raise_rows(batch):
         place = tile_of(chip if batch == 0 else 1 - chip, half_rows)
@@ -426,15 +423,14 @@
     gather_finish(0, 0, group_view, (1,))
     weight_wait(0, w_up_far, w_up)
     raise_rows(0)
-    gather_relay(0, 0, group_view)
-    gather_finish(0, 0, group_view, (2,))
-    raise_rows(1)
 
     far_half = 1 - mine // (seq_size // 2)
 
     def head_copy(k, h):
-        if k == 6:
-            src, place = outbox.at[3, h], own_rows
+        if k >= 6:
+            start = half_rows * (7 - k)
+            src = outbox.at[3, h, start : start + half_rows]
+            place = tile_of(2 * mine + 7 - k, half_rows)
         else:
             a, batch = k // 2, k % 2
             piece = 1 - chip if batch == 0 else chip
@@ -442,7 +438,7 @@
             place = tile_of(2 * mine + piece, half_rows)
         return remote(
             src,
-            heads.at[3 if k == 6 else k // 2, place],
+            heads.at[min(k // 2, 3), place],
             out_send.at[k],
             out_recv.at[k],
             {"seq": h},
@@ -466,8 +462,24 @@
             def _():
                 outbox[a, h, pl.ds(pl.multiple_of(start, size), size), :] = part
 
-    def tile_order(jj):
-        return lax.rem(far_half * (tiles // 2) + jj, tiles)
+    def d_attn_tile(upper, jj):
+        j = far_half if jj == 0 else 1 - far_half
+        start = 0 if upper else half_rows
+        acc = jnp.zeros((half_rows, wide_tile), WIDE)
+        for q in range(tp_size):
+            acc += dot_last(
+                wide_grad[q, start : start + half_rows],
+                w_out[tile_of(j, wide_tile), q * columns : (q + 1) * columns],
+            )
+        held = wide_tile // HEAD_DIM
+        keep_heads(3, j * held, acc.astype(LOW), start, half_rows)
+        if upper:
+            for u in range(held):
+                start_head(7, j * held + u)
+
+    def d_attn_rows(upper):
+        for jj in range(2):
+            d_attn_tile(upper, jj)
 
     def relay_rows(batch):
         for j in range(2):
@@ -505,6 +517,13 @@
 
         lax.fori_loop(0, steps, step, 0)
 
+    gather_relay(1, 1, grad_views[0])
+    gather_relay(0, 0, group_view)
+    weight_wait(4, w_out_far, w_out)
+    gather_finish(1, 1, grad_views[0])
+    d_attn_tile(1, 0)
+    gather_finish(0, 0, group_view, (2,))
+    raise_rows(1)
     near_copies[3].wait()
     relay_rows(0)
     for j in range(2):
@@ -513,8 +532,9 @@
     norm_rows(0)
     weight_wait(1, w_key_far, w_key)
     project(1, w_key, 0, tile)
+    d_attn_tile(1, 1)
     relay_rows(1)
-    gather_start(1, 1, grad_view)
+    gather_start(6, 1, grad_views[1])
     weight_wait(2, w_query_far, w_query)
     project(0, w_query, 0, wide_tile)
     weight_wait(3, w_value_far, w_value)
@@ -525,54 +545,48 @@
     norm_rows(1)
     project(1, w_key, 1, wide_tile)
     project(0, w_query, 1, wide_tile)
-    gather_relay(1, 1, grad_view)
+    gather_relay(6, 1, grad_views[1])
     project(2, w_value, 1, wide_tile)
-    weight_wait(4, w_out_far, w_out)
-    gather_finish(1, 1, grad_view)
-
-    def d_attn_step(jj, carry):
-        j = tile_order(jj)
-        acc = jnp.zeros((rows, tile), WIDE)
-        for q in range(tp_size):
-            acc += dot_last(
-                wide_grad[q], w_out[tile_of(j, tile), q * columns : (q + 1) * columns]
-            )
-        keep_heads(3, 2 * j, acc.astype(LOW), 0, rows)
-        for u in range(2):
-            start_head(6, 2 * j + u)
-        return carry
-
-    lax.fori_loop(0, tiles, d_attn_step, 0)
-
+    gather_finish(6, 1, grad_views[1])
+
+    d_attn_rows(0)
 
     def heads_arrived(k):
-        size = (rows if k == 6 else half_rows) * (seq_size - 1)
-        place = heads.at[3 if k == 6 else k // 2, :size]
+        place = heads.at[min(k // 2, 3), : half_rows * (seq_size - 1)]
         remote(place, place, out_send.at[k], out_recv.at[k], {"seq": mine}).wait_recv()
 
-    def turn_square(q, carry):
-        steps = columns // tile
-        for i in range(steps):
-            for j in range(i, steps):
-                upper = w_key.at[tile_of(q * steps + i, tile), j * tile : (j + 1) * tile]
-                lower = w_key.at[tile_of(q * steps + j, tile), i * tile : (i + 1) * tile]
-                turned = upper[...].T
-                if i != j:
-                    upper[...] = lower[...].T
-                lower[...] = turned
-        return carry
-
-    lax.fori_loop(0, tp_size, turn_square, 0)
+    def turn(weight):
+        def turn_square(q, carry):
+            square = weight.at[tile_of(q, columns)]
+            square[...] = square[...].T
+            return carry
+
+        lax.fori_loop(0, tp_size, turn_square, 0)
+
+    index = lax.broadcasted_iota(jnp.int32, (patches_total, shards), 0)
+    lane = lax.broadcasted_iota(jnp.int32, (patches_total, shards), 1)
+    owner = jnp.where((index >= lane * cap) & (index < lane * cap + cap), 1.0, 0.0).astype(LOW)
+    valid = jnp.where(starts[...].astype(WIDE) < limit, 1.0, 0.0).astype(LOW)
+    spread = dot(owner, valid)
+    slots = lax.broadcasted_iota(jnp.int32, (patches_total, cap), 1)
+    places_in = lax.broadcasted_iota(jnp.int32, (patches_total, cap), 0)
+    valid_column = jnp.sum(
+        jnp.where(jnp.bitwise_and(places_in, cap - 1) == slots, spread, 0.0), 1, keepdims=True
+    )
+    key_bias[...] = jnp.broadcast_to((valid_column - 1.0) * -NEG, key_bias.shape)
+    turn(w_key)
     for k in range(4):
         heads_arrived(k)
+    for step in range(seq_size):
+        start_head(6, lax.rem(far_half * (seq_size // 2) + step, seq_size))
 
     blocks = patches_total // tile
     own_columns = tile_of(mine, HEAD_DIM)
 
     def piece_of(k):
-        if k < 3:
+        if k < 2:
             return k, 0, rows
-        return 3, half_rows * (k - 3), half_rows
+        return 2 + k % 2, half_rows * (k // 2 - 1), half_rows
 
     half_seq = seq_size // 2
     near_half = mine // half_seq
@@ -674,13 +688,17 @@
     for i in ends:
         mix(i)
         send_back(0, i)
+    turn(w_query)
+    heads_arrived(7)
     heads_arrived(6)
     for i in reversed(range(blocks)):
         attend_back(i)
         send_back(1, i)
+    turn(w_value)
     sent_back(0)
-    for i in reversed(range(blocks)):
-        send_back(2, i)
+    for k in (2, 3):
+        for i in range(blocks):
+            send_back(k, i)
 
     def returns_arrived(k, sides=(0, 1)):
         a, start, size = piece_of(k)
@@ -746,8 +764,6 @@
             partial[0, quarter, :, here] = dot(back[0], w_out[:, at]).astype(LOW)
         if k % 2 == 0:
             pair_copy(0, k // 2).start()
-    weights = {1: w_query, 2: w_value, 3: w_key}
-
     def dots_copy(half, offset):
         return remote(
             dots_out.at[half],
@@ -794,48 +810,52 @@
         )
 
     half_columns = columns // 2
-    for a, side in ((1, 0), (1, 1), (2, 0), (2, 1)):
-        returns_arrived(a, (side,))
-        sources = tile_of(near_half if side == 0 else 1 - near_half, half_columns)
-
-        def quarter_step(quarter, carry):
-            for j in range(tiles):
-                at = tile_of(quarter * tiles + j, tile)
-                here = tile_of(j, tile)
-                more = dot_last(back[a, :, sources], weights[a][at, sources])
-                if a == 1 and side == 0:
+    for side in range(2):
+        returns_arrived(1, (side,))
+        which = near_half if side == 0 else 1 - near_half
+
+        def query_step(quarter, carry):
+            at = tile_of(quarter * 2 + which, half_columns)
+            for j in range(2):
+                here = slice(j * wide_tile, (j + 1) * wide_tile)
+                more = dot(back[1, :, tile_of(which, half_columns)], w_query[at, here])
+                if side == 0:
                     grad_sum[quarter, :, here] = more
                 else:
                     grad_sum[quarter, :, here] += more
             return carry
 
-        lax.fori_loop(0, tp_size, quarter_step, 0, unroll=2)
-        if a == 1 and side == 0:
-            sent_back(1)
-            for i in reversed(range(blocks)):
-                send_back(3, i)
+        lax.fori_loop(0, tp_size, query_step, 0, unroll=2)
+        sent_back(1 + side)
+        for i in range(blocks):
+            send_back(4 + side, i)
+        if side == 0:
             cross_over(0)
-        if a == 1 and side == 1:
-            sent_back(2)
-            for i in reversed(range(blocks)):
-                send_back(4, i)
+
+    def half_gradient(half):
+        part = stages[1 + half][1]
+
+        def value_step(quarter, carry):
+            for j in range(2):
+                here = slice(j * wide_tile, (j + 1) * wide_tile)
+                turned = w_value[tile_of(quarter, columns), here]
+                grad_sum[quarter, part, here] += dot(back[2, part], turned)
+            return carry
+
+        def product(quarter, here):
+            turned = w_key[tile_of(quarter, columns), here]
+            return grad_sum[quarter, part, here] + dot(back[3, part], turned)
+
+        returns_arrived(2 + 2 * half)
+        lax.fori_loop(0, tp_size, value_step, 0, unroll=2)
+        returns_arrived(3 + 2 * half)
+        return share_gradient(half, product)
+
+    upper_dots = half_gradient(0)
+    lower_dots = half_gradient(1)
     out_value[...] = jnp.where(
         row_valid > 0.5, wide[t].astype(WIDE) + summed(0), 0.0
     ).astype(LOW)
-
-    def product_of(half):
-        part = stages[1 + half][1]
-
-        def product(quarter, here):
-            turned = w_key[tile_of(quarter, columns), here]
-            return grad_sum[quarter, part, here] + dot(back[3, part], turned)
-
-        return product
-
-    returns_arrived(3)
-    upper_dots = share_gradient(0, product_of(0))
-    returns_arrived(4)
-    lower_dots = share_gradient(1, product_of(1))
     finish_gradient(0, upper_dots)
     finish_gradient(1, lower_dots)
 
@@ -845,10 +865,10 @@
 
     for kind, sent in ((0, group.at[: 3 * cap]), (1, wide_grad.at[:3]), (2, wide.at[:3])):
         gather_copy(0, 0, kind, sent).wait_send()
-    for k in range(7):
-        sent = outbox.at[3, 1:] if k == 6 else outbox.at[k // 2, 1:, :half_rows]
+    for k in range(8):
+        sent = outbox.at[min(k // 2, 3), 1:, :half_rows]
         remote(sent, sent, out_send.at[k], out_recv.at[k], {"seq": mine}).wait_send()
-    for k in (3, 4):
+    for k in (3, 4, 5):
         sent_back(k)
     for stage in range(len(stages)):
         a, part = stages[stage]
@@ -888,7 +908,6 @@
         pltpu.VMEM((tp_size, rows, columns), LOW),
         pltpu.VMEM((tp_size, rows, columns), LOW),
         pltpu.VMEM((tp_size, rows, columns), LOW),
-        pltpu.VMEM((total, 1), WIDE),
         pltpu.VMEM((total, 128), WIDE),
         pltpu.VMEM((rows, 1), WIDE),
         pltpu.VMEM((4, seq_size, rows, HEAD_DIM), LOW),
@@ -913,11 +932,11 @@
         dma((4,)),
         dma((2,)),
         dma((3,)),
-        dma((3, 6)),
-        dma((7,)),
-        dma((7,)),
-        dma((5,)),
-        dma((5, 2)),
+        dma((3, 7)),
+        dma((8,)),
+        dma((8,)),
+        dma((6,)),
+        dma((6, 2)),
         dma((3,)),
         dma((3, 2)),
         dma((3,)),

time: 74.6 us -> 73.3 us (0.983)
  Pallas kernels: 72.2 us -> 70.9 us
    pallas_call x1, Pallas kernels: 72.2 us -> 70.9 us  [per_device_whole(): pl.pallas_call(functools.partial(layer_kernel, seq_size, tp_size), out_sh...]
where the time goes in v4:
time: 73.3 us; the launch traced here: 73 us
  Pallas kernels  70.9 us (97%)
  local copies, waits for them, and re-layouts  1.5 us (2%)
    pallas_call x1, Pallas kernels, per_device_whole(): pl.pallas_call(functools.partial(layer_kernel, seq_size, tp_size), out_sh...  70.9 us
    unnamed x2, local copies, waits for them, and re-layouts  1.5 us

profile of v4, /device:TPU:0, one launch (start us, length us, event | category | flops | bytes accessed | tf_op | source)
XLA Modules:
  0.0 73.0 jit_solution(7238866264296460686)
XLA Ops:
  0.6 70.9 %shard_map.104 = (bf16[128,1024]{1,0:T(8,128)(2,1)S(1)}, f32[128,1024]{1,0:T(8,128)S(1)}) custom-call(s32[32,32]{1,0:T(8,128)} %starts_far.1, f32[1,4096]{1,0:T(1,128)} %bitcast.1, bf16[256,1280]{1,0:T(8,128)(2,1)} %encoded_far.1, bf16[128,1024]{1,0:T(8,128)(2,1)} %cotangent_far.1, bf16[1280,1024]{1,0:T(8,128)(2,1)} %w_up_far.1, ...), custom_call_target="tpu_custom_call" | custom-call | tf_op jit(solution)/shard_map/pallas_call | solution.py:950
  71.5 0.7 copy.13
  72.2 0.8 %copy.14 = f32[128,1024]{1,0:T(8,128)} copy(f32[128,1024]{1,0:T(8,128)S(1)} %get-tuple-element.3) | data formatting | bytes 1048576

commit v5 on v4

--- a/solution.py
+++ b/solution.py
@@ -574,11 +574,12 @@
         jnp.where(jnp.bitwise_and(places_in, cap - 1) == slots, spread, 0.0), 1, keepdims=True
     )
     key_bias[...] = jnp.broadcast_to((valid_column - 1.0) * -NEG, key_bias.shape)
-    turn(w_key)
-    for k in range(4):
+    for k in (2, 3, 0):
         heads_arrived(k)
     for step in range(seq_size):
         start_head(6, lax.rem(far_half * (seq_size // 2) + step, seq_size))
+    turn(w_key)
+    heads_arrived(1)
 
     blocks = patches_total // tile
     own_columns = tile_of(mine, HEAD_DIM)
@@ -688,17 +689,18 @@
     for i in ends:
         mix(i)
         send_back(0, i)
-    turn(w_query)
     heads_arrived(7)
     heads_arrived(6)
     for i in reversed(range(blocks)):
         attend_back(i)
+    for i in range(blocks):
         send_back(1, i)
     turn(w_value)
     sent_back(0)
     for k in (2, 3):
         for i in range(blocks):
             send_back(k, i)
+    turn(w_query)
 
     def returns_arrived(k, sides=(0, 1)):
         a, start, size = piece_of(k)

time: 73.3 us -> 72.7 us (level)
  no operation moved by 1% of the time
where the time goes in v5:
time: 72.7 us; the launch traced here: 72.4 us
  Pallas kernels  70.3 us (97%)
  local copies, waits for them, and re-layouts  1.5 us (2%)
    pallas_call x1, Pallas kernels, per_device_whole(): pl.pallas_call(functools.partial(layer_kernel, seq_size, tp_size), out_sh...  70.3 us
    unnamed x2, local copies, waits for them, and re-layouts  1.5 us

profile of v5, /device:TPU:0, one launch (start us, length us, event | category | flops | bytes accessed | tf_op | source)
XLA Modules:
  0.0 72.4 jit_solution(18231890653532189501)
XLA Ops:
  0.6 70.3 %shard_map.104 = (bf16[128,1024]{1,0:T(8,128)(2,1)S(1)}, f32[128,1024]{1,0:T(8,128)S(1)}) custom-call(s32[32,32]{1,0:T(8,128)} %starts_far.1, f32[1,4096]{1,0:T(1,128)} %bitcast.1, bf16[256,1280]{1,0:T(8,128)(2,1)} %encoded_far.1, bf16[128,1024]{1,0:T(8,128)(2,1)} %cotangent_far.1, bf16[1280,1024]{1,0:T(8,128)(2,1)} %w_up_far.1, ...), custom_call_target="tpu_custom_call" | custom-call | tf_op jit(solution)/shard_map/pallas_call | solution.py:952
  70.9 0.7 copy.13
  71.6 0.8 %copy.14 = f32[128,1024]{1,0:T(8,128)} copy(f32[128,1024]{1,0:T(8,128)S(1)} %get-tuple-element.3) | data formatting | bytes 1048576

commit v6 on v5

--- a/solution.py
+++ b/solution.py
@@ -784,7 +784,7 @@
             for j in range(2):
                 at = tile_of(quarter * 2 + j, wide_tile)
                 here = slice(j * wide_tile, (j + 1) * wide_tile)
-                whole = product(quarter, here)
+                whole = product(k, here)
                 partial[1, quarter, part, here] = whole.astype(LOW)
                 inner = gain[:, at] * whole * wide[quarter, part, here].astype(WIDE)
                 dots += jnp.sum(inner, 1, keepdims=True)
@@ -837,19 +837,21 @@
     def half_gradient(half):
         part = stages[1 + half][1]
 
-        def value_step(quarter, carry):
+        def value_product(quarter, here):
+            return dot(back[2, part], w_value[tile_of(quarter, columns), here])
+
+        def product(k, here):
+            quarter = order[k]
+            whole = grad_sum[quarter, part, here]
+            if k >= 2:
+                whole += value_product(quarter, here)
+            return whole + dot(back[3, part], w_key[tile_of(quarter, columns), here])
+
+        returns_arrived(2 + 2 * half)
+        for k in range(2):
             for j in range(2):
                 here = slice(j * wide_tile, (j + 1) * wide_tile)
-                turned = w_value[tile_of(quarter, columns), here]
-                grad_sum[quarter, part, here] += dot(back[2, part], turned)
-            return carry
-
-        def product(quarter, here):
-            turned = w_key[tile_of(quarter, columns), here]
-            return grad_sum[quarter, part, here] + dot(back[3, part], turned)
-
-        returns_arrived(2 + 2 * half)
-        lax.fori_loop(0, tp_size, value_step, 0, unroll=2)
+                grad_sum[order[k], part, here] += value_product(order[k], here)
         returns_arrived(3 + 2 * half)
         return share_gradient(half, product)
 

time: 72.7 us -> 72.7 us (level)
  no operation moved by 1% of the time
where the time goes in v6:
time: 72.7 us; the launch traced here: 72.4 us
  Pallas kernels  70.3 us (97%)
  local copies, waits for them, and re-layouts  1.5 us (2%)
    pallas_call x1, Pallas kernels, per_device_whole(): pl.pallas_call(functools.partial(layer_kernel, seq_size, tp_size), out_sh...  70.3 us
    unnamed x2, local copies, waits for them, and re-layouts  1.5 us

profile of v6, /device:TPU:0, one launch (start us, length us, event | category | flops | bytes accessed | tf_op | source)
XLA Modules:
  0.0 72.4 jit_solution(5697226745388699160)
XLA Ops:
  0.6 70.3 %shard_map.104 = (bf16[128,1024]{1,0:T(8,128)(2,1)S(1)}, f32[128,1024]{1,0:T(8,128)S(1)}) custom-call(s32[32,32]{1,0:T(8,128)} %starts_far.1, f32[1,4096]{1,0:T(1,128)} %bitcast.1, bf16[256,1280]{1,0:T(8,128)(2,1)} %encoded_far.1, bf16[128,1024]{1,0:T(8,128)(2,1)} %cotangent_far.1, bf16[1280,1024]{1,0:T(8,128)(2,1)} %w_up_far.1, ...), custom_call_target="tpu_custom_call" | custom-call | tf_op jit(solution)/shard_map/pallas_call | solution.py:954
  70.9 0.7 copy.13
  71.7 0.8 %copy.14 = f32[128,1024]{1,0:T(8,128)} copy(f32[128,1024]{1,0:T(8,128)S(1)} %get-tuple-element.3) | data formatting | bytes 1048576

commit v7 on v6

--- a/solution.py
+++ b/solution.py
@@ -532,7 +532,6 @@
     norm_rows(0)
     weight_wait(1, w_key_far, w_key)
     project(1, w_key, 0, tile)
-    d_attn_tile(1, 1)
     relay_rows(1)
     gather_start(6, 1, grad_views[1])
     weight_wait(2, w_query_far, w_query)
@@ -549,6 +548,7 @@
     project(2, w_value, 1, wide_tile)
     gather_finish(6, 1, grad_views[1])
 
+    d_attn_tile(1, 1)
     d_attn_rows(0)
 
     def heads_arrived(k):

time: 72.7 us -> 72.3 us (level)
  no operation moved by 1% of the time
where the time goes in v7:
time: 72.3 us; the launch traced here: 72 us
  Pallas kernels  69.9 us (97%)
  local copies, waits for them, and re-layouts  1.5 us (2%)
    pallas_call x1, Pallas kernels, per_device_whole(): pl.pallas_call(functools.partial(layer_kernel, seq_size, tp_size), out_sh...  69.9 us
    unnamed x2, local copies, waits for them, and re-layouts  1.5 us

profile of v7, /device:TPU:0, one launch (start us, length us, event | category | flops | bytes accessed | tf_op | source)
XLA Modules:
  0.0 72.0 jit_solution(10819863683941283977)
XLA Ops:
  0.6 69.9 %shard_map.104 = (bf16[128,1024]{1,0:T(8,128)(2,1)S(1)}, f32[128,1024]{1,0:T(8,128)S(1)}) custom-call(s32[32,32]{1,0:T(8,128)} %starts_far.1, f32[1,4096]{1,0:T(1,128)} %bitcast.1, bf16[256,1280]{1,0:T(8,128)(2,1)} %encoded_far.1, bf16[128,1024]{1,0:T(8,128)(2,1)} %cotangent_far.1, bf16[1280,1024]{1,0:T(8,128)(2,1)} %w_up_far.1, ...), custom_call_target="tpu_custom_call" | custom-call | tf_op jit(solution)/shard_map/pallas_call | solution.py:954
  70.5 0.7 copy.13
  71.2 0.8 %copy.14 = f32[128,1024]{1,0:T(8,128)} copy(f32[128,1024]{1,0:T(8,128)S(1)} %get-tuple-element.3) | data formatting | bytes 1048576
